TPU v7x, 32 devices: a whole 2x2x4 slice. The times are simulated.
32 devices in a mesh: rows: 8 (over z, y), feat: 4 (over x, core).
Axes of the slice: x: 2, y: 2, z: 4, core: 2. Of those that a mesh axis runs over, the one named last changes fastest.
Arguments:
- features: float32 [100, 8192], P('feat', 'rows'), may hold values from -12 to 12
- tiles: float32 [1024, 128, 128], P('rows'), may hold values from 0 to 1.5
- tile_slot: int32 [1024], P('rows'), may hold values from 0 to 15, as said below
- send_blocks: int32 [8, 8, 1], P('rows'), may hold values from 0 to 7
Outputs:
- ranked: float32 [100, 8192], P('feat', 'rows')
- change: float32 [4], replicated
Inputs may be any that keep to these rules, and one draw needn't show every extreme that they name: `tile_slot`: among the tiles of one index of rows, every received slot (8 to 15) is named by at least one tile.
All inputs are finite; a program needn't handle non-finite values.
Results may differ from a plain program's by a relative error of at most 0.0001.
Values sent between devices are 32-bit elements; how exact they have to be, the bound alone decides.
No kernel may reach another device: no remote copies, remote signals or barrier semaphores. Data moves between devices by JAX's collectives and lax.ppermute only.
A program may use at most 128 MiB of HBM per device.

v0:
```python
import jax
import jax.numpy as jnp
from jax import lax
from jax.sharding import PartitionSpec as P

ITERS = 4


teleport = 0.15


def shards(features, tiles, tile_slot, send_blocks):
    width_dev, node_count = features.shape
    tile_size = tiles.shape[1]
    block_count = node_count // tile_size
    per_block = tiles.shape[0] // block_count
    peer_count = lax.axis_size("rows")
    slot_count = send_blocks.shape[2]
    total_nodes = node_count * peer_count
    total_width = width_dev * lax.axis_size("feat")
    degree = 1.0 + jnp.sum(tiles, axis=2).reshape(block_count, per_block, tile_size).sum(axis=1)
    start = features.reshape(width_dev, block_count, tile_size).transpose(1, 0, 2)
    outgoing_ids = send_blocks[0].reshape(-1)
    current = start
    partials = []
    for iteration in range(ITERS):
        outgoing = current[outgoing_ids].reshape(peer_count, slot_count, width_dev, tile_size)
        received = lax.all_to_all(outgoing, "rows", split_axis=0, concat_axis=0, tiled=True)
        halo = received.reshape(peer_count * slot_count, width_dev, tile_size)
        buffer = jnp.concatenate([current, halo], axis=0)
        picked = buffer[tile_slot]
        product = jnp.einsum("tij,tfj->tfi", tiles, picked, precision=lax.Precision.HIGHEST)
        summed = product.reshape(block_count, per_block, width_dev, tile_size).sum(axis=1)
        updated = (1.0 - teleport) * (current + summed) / degree[:, None, :] + teleport * start
        partial_value = jnp.sum((updated - current) ** 2) / (total_width * total_nodes)
        partials.append(lax.psum(partial_value, ("rows", "feat")))
        current = updated
    change = jnp.stack(partials)
    ranked = current.transpose(1, 0, 2).reshape(width_dev, node_count)
    return (ranked, change)


def solution(mesh):
    return jax.shard_map(
        shards,
        mesh=mesh,
        in_specs=(P("feat", "rows"), P("rows", None, None), P("rows"), P("rows", None, None)),
        out_specs=(P("feat", "rows"), P()),
        check_vma=False,
    )
```

profile of v0, /device:TPU:0, one launch (start us, length us, event | category | flops | bytes accessed | tf_op | source)
XLA Modules:
  0.0 164.5 jit_solution(2037960440983145954)
XLA Ops:
  0.6 0.7 fusion.12
  1.3 0.9 copy.87
  2.3 0.6 gather_fusion
  2.8 0.7 copy.67
  3.6 7.3 %all-to-all-start = ((f32[8,1,25,128]{3,1,2,0:T(1,128)}), f32[8,1,25,128]{3,1,2,0:T(1,128)S(1)}, u32[]{:S(2)}, u32[]{:S(2)}) async-start(f32[8,1,25,128]{3,1,2,0:T(1,128)} %copy.67), calls=%async_computation | async-start | bytes 204800 | tf_op jit(solution)/shard_map/all_to_all | solution.py:28
  10.9 0.7 compare_select_fusion
  11.6 5.6 %reduce_sum.100 = f32[128,128]{1,0:T(8,128)S(1)} reduce(f32[128,128,128]{2,1,0:T(8,128)} %param.5, f32[]{:T(128)} %constant.6.clone.1), dimensions={2}, to_apply=%region_1.0 | reduce | flops 2080768 | bytes 8454148 | tf_op jit(solution)/shard_map/reduce_sum | solution.py:21
  17.2 0.8 all-to-all-done
  18.1 0.8 gather_fusion.1
  18.9 15.4 %bitcast_reduce_fusion.3 = f32[8,25,128]{2,1,0:T(8,128)S(1)} fusion(f32[128,25,128]{2,1,0:T(8,128)S(1)} %gather_fusion.1, f32[128,128,128]{2,1,0:T(8,128)} %param.5), kind=kOutput, calls=%fused_computation.11 | convolution fusion | flops 629529600 | bytes 10129408 | tf_op jit(solution)/shard_map/tij,tfj->tfi/dot_general | solution.py:32
  35.0 12.1 %all_to_all.20 = f32[8,1,25,128]{3,1,2,0:T(1,128)S(1)} all-to-all(f32[8,1,25,128]{3,1,2,0:T(1,128)S(1)} %copy.71), channel_id=1, replica_groups=mesh['rows'=8,'feat'=4] {'rows'}, dimensions={0} | all-to-all | bytes 204800 | tf_op jit(solution)/shard_map/all_to_all | solution.py:28
  47.2 0.8 gather_fusion.3
  48.0 15.4 %bitcast_reduce_fusion.2 = f32[8,25,128]{2,1,0:T(8,128)S(1)} fusion(f32[128,25,128]{2,1,0:T(8,128)S(1)} %gather_fusion.3, f32[128,128,128]{2,1,0:T(8,128)} %param.5), kind=kOutput, calls=%fused_computation.10 | convolution fusion | flops 629529600 | bytes 10129408 | tf_op jit(solution)/shard_map/tij,tfj->tfi/dot_general | solution.py:32
  63.4 0.6 gather_fusion.4
  64.1 9.5 %all_to_all.21 = f32[8,1,25,128]{3,1,2,0:T(1,128)S(1)} all-to-all(f32[8,1,25,128]{3,1,2,0:T(1,128)S(1)} %copy.75), channel_id=1, replica_groups=mesh['rows'=8,'feat'=4] {'rows'}, dimensions={0} | all-to-all | bytes 204800 | tf_op jit(solution)/shard_map/all_to_all | solution.py:28
  73.7 0.8 gather_fusion.5
  74.5 15.4 %bitcast_reduce_fusion.1 = f32[8,25,128]{2,1,0:T(8,128)S(1)} fusion(f32[128,25,128]{2,1,0:T(8,128)S(1)} %gather_fusion.5, f32[128,128,128]{2,1,0:T(8,128)} %param.5), kind=kOutput, calls=%fused_computation.9 | convolution fusion | flops 629529600 | bytes 10129408 | tf_op jit(solution)/shard_map/tij,tfj->tfi/dot_general | solution.py:32
  90.6 9.5 %all_to_all.22 = f32[8,1,25,128]{3,1,2,0:T(1,128)S(1)} all-to-all(f32[8,1,25,128]{3,1,2,0:T(1,128)S(1)} %copy.79), channel_id=1, replica_groups=mesh['rows'=8,'feat'=4] {'rows'}, dimensions={0} | all-to-all | bytes 204800 | tf_op jit(solution)/shard_map/all_to_all | solution.py:28
  100.2 0.8 gather_fusion.7
  101.0 15.4 %bitcast_reduce_fusion = f32[8,25,128]{2,1,0:T(8,128)S(1)} fusion(f32[128,25,128]{2,1,0:T(8,128)S(1)} %gather_fusion.7, f32[128,128,128]{2,1,0:T(8,128)} %param.5), kind=kOutput, calls=%fused_computation.8 | convolution fusion | flops 629529600 | bytes 10129408 | tf_op jit(solution)/shard_map/tij,tfj->tfi/dot_general | solution.py:32
  116.4 0.7 multiply_reduce_fusion.3
  119.9 0.7 copy.88
  120.6 40.9 %all-reduce = (f32[1]{0:T(128)}, f32[1]{0:T(128)}, f32[1]{0:T(128)}, f32[1]{0:T(128)}) all-reduce(f32[1]{0:T(128)} %bitcast.27, f32[1]{0:T(128)} %bitcast.26, f32[1]{0:T(128)} %bitcast.25, f32[1]{0:T(128)} %bitcast.24), channel_id=1, replica_groups=mesh['rows'=8,'feat'=4] {'rows','feat'}, use_global_device_ids=true, to_apply=%region_13.0 | all-reduce | flops 4 | bytes 32 | tf_op jit(solution)/shard_map/psum | solution.py:36
  161.5 3.0 %pad_maximum_fusion.4 = f32[4]{0:T(128)} fusion(f32[1]{0:T(128)} %get-tuple-element.6, f32[1]{0:T(128)} %get-tuple-element.7, f32[1]{0:T(128)} %get-tuple-element.8, f32[1]{0:T(128)} %get-tuple-element.9), kind=kLoop, calls=%fused_computation.51 | loop fusion | flops 12 | bytes 32 | tf_op jit(solution)/shard_map/stack | solution.py:38
  (24 shorter events, 2.1 us)
Async XLA Ops:
  3.6 14.5 %all-to-all-start = ((f32[8,1,25,128]{3,1,2,0:T(1,128)}), f32[8,1,25,128]{3,1,2,0:T(1,128)S(1)}, u32[]{:S(2)}, u32[]{:S(2)}) async-start(f32[8,1,25,128]{3,1,2,0:T(1,128)} %copy.67), calls=%async_computation | async-start | bytes 204800 | tf_op jit(solution)/shard_map/all_to_all | solution.py:28
where the time goes:
time: 165 us; the launch traced here: 164 us
  blocking collectives  72.1 us (44%)
  matrix products  61.5 us (37%)
  other arithmetic  11.2 us (7%)
  local copies, waits for them, and re-layouts  8.15 us (5%)
  starting transfers between devices  7.31 us (4%)
  between operations  3.33 us (2%)
    dot_general x4, matrix products, shards(): jnp.einsum('tij,tfj->tfi', tiles, picked, precision=lax.Precision.HIGHEST)  61.5 us
    psum x1, blocking collectives, shards(): partials.append(lax.psum(partial_value, ('rows', 'feat')))  40.9 us
    all_to_all x3, blocking collectives, shards(): lax.all_to_all(outgoing, 'rows', split_axis=0, concat_axis=0, tiled=True)  31.2 us
    all_to_all x1, starting transfers between devices, shards(): lax.all_to_all(outgoing, 'rows', split_axis=0, concat_axis=0, tiled=True)  7.31 us
    reduce_sum x2, other arithmetic, shards(): jnp.sum(tiles, axis=2).reshape(block_count, per_block, tile_size)  5.63 us
  transfers between devices with their start and end apart: 1, of which 1 were waited for; matrix products, arithmetic and copies ran while one was open for 4% of the time, Pallas kernels for 0%

commit v1 on v0

v1 whole, which is shorter than its diff:
```python
import jax
import jax.numpy as jnp
from jax import lax
from jax.experimental import pallas as pl
from jax.experimental.pallas import tpu as pltpu
from jax.sharding import PartitionSpec as P

ITERS = 4


teleport = 0.15

VMEM, SMEM = pltpu.VMEM, pltpu.SMEM
WHOLE = pl.BlockSpec(memory_space=VMEM)
SCALARS = pl.BlockSpec(memory_space=SMEM)
LIMIT = pltpu.CompilerParams(vmem_limit_bytes=20 * 1024 * 1024)


def framed(block, rows):
    width, tile = block.shape
    row = lax.broadcasted_iota(jnp.int32, (rows - width, tile), 0)
    return jnp.concatenate([block, jnp.where(row == 0, 1.0, 0.0).astype(block.dtype)], axis=0)


def split(v):
    high = v.astype(jnp.bfloat16)
    return high, (v - high.astype(jnp.float32)).astype(jnp.bfloat16)


def begin_kernel(features_ref, ids_ref, start_ref, outgoing_ref):
    blocks, rows, tile = start_ref.shape
    width = features_ref.shape[0]
    for b in range(blocks):
        start_ref[b] = framed(features_ref[:, b * tile:(b + 1) * tile], rows)
    for d in range(outgoing_ref.shape[0]):
        at = pl.multiple_of(ids_ref[d] * tile, tile)
        outgoing_ref[d] = features_ref[:, pl.ds(at, tile)]


def step_kernel(index, refs):
    first, last = index == 0, index == ITERS - 1
    refs = list(refs)
    current_ref, received_ref, start_ref, slot_ref, ids_ref = refs[:5]
    views_ref = refs.pop()
    if first:
        tiles_ref, next_ref, outgoing_ref, sums_ref, scale_ref, weights_ref = refs[5:]
    elif last:
        scale_ref, weights_ref, past_ref, ranked_ref, sums_ref = refs[5:]
    else:
        scale_ref, weights_ref, past_ref, next_ref, outgoing_ref, sums_ref = refs[5:]
    blocks, rows, tile = current_ref.shape
    width = received_ref.shape[1]
    per_block = weights_ref.shape[0] // (blocks * tile)
    for c in range(blocks + received_ref.shape[0]):
        v = current_ref[c] if c < blocks else framed(received_ref[c - blocks], rows)
        views_ref[c, 0:rows], views_ref[c, rows:2 * rows] = split(v)
    square = jnp.zeros((8, tile), jnp.float32)
    for b in range(blocks):
        if first:
            for t in range(b * per_block, (b + 1) * per_block):
                high, low = split(tiles_ref[t].T)
                weights_ref[t * tile:(t + 1) * tile, 0:tile] = high
                weights_ref[t * tile:(t + 1) * tile, tile:2 * tile] = low
        picked = [views_ref[slot_ref[t]] for t in range(b * per_block, (b + 1) * per_block)]
        s = jnp.dot(
            jnp.concatenate(picked, axis=1),
            weights_ref[b * per_block * tile:(b + 1) * per_block * tile, :],
            preferred_element_type=jnp.float32,
        )
        s = s[0:rows] + s[rows:2 * rows]
        s = s[:, 0:tile] + s[:, tile:2 * tile]
        r = slice(b * tile, (b + 1) * tile)
        if first:
            scale = (1.0 - teleport) / (1.0 + s[width:width + 1])
            scale_ref[:, r] = scale
        else:
            scale = scale_ref[:, r]
        old = current_ref[b]
        new = (old + s) * scale + teleport * start_ref[b]
        row = lax.broadcasted_iota(jnp.int32, (rows, tile), 0)
        new = jnp.where(row < width, new, start_ref[b])
        d = new - old
        d = d * d
        for k in range(rows // 8):
            square = square + d[8 * k:8 * k + 8]
        if last:
            ranked_ref[:, r] = new[0:width]
        else:
            next_ref[b] = new
    row = lax.broadcasted_iota(jnp.int32, (8, tile), 0)
    sums = jnp.where(row == index, jnp.sum(square, axis=0, keepdims=True), 0.0 if first else past_ref[...])
    if last:
        lane = lax.broadcasted_iota(jnp.int32, (8, tile), 1)
        sums = jnp.where(row == lane, jnp.sum(sums, axis=1, keepdims=True), 0.0)
        sums_ref[...] = jnp.broadcast_to(jnp.sum(sums, axis=0, keepdims=True), sums_ref.shape)
    else:
        sums_ref[...] = sums
    if not last:
        for d in range(outgoing_ref.shape[0]):
            outgoing_ref[d] = next_ref[ids_ref[d], 0:width]


def shards(features, tiles, tile_slot, send_blocks):
    width, node_count = features.shape
    tile_count, tile, _ = tiles.shape
    blocks = node_count // tile
    peers = lax.axis_size("rows")
    lanes = lax.axis_size("feat")
    halo = peers * send_blocks.shape[2]
    rows = -(-(width + 1) // 8) * 8
    f32 = jnp.float32
    ids = send_blocks.reshape(-1)
    shape = jax.ShapeDtypeStruct

    start, outgoing = pl.pallas_call(
        begin_kernel,
        out_shape=(shape((blocks, rows, tile), f32), shape((halo, width, tile), f32)),
        in_specs=[WHOLE, SCALARS],
        out_specs=(WHOLE, WHOLE),
        compiler_params=LIMIT,
        cost_estimate=pl.CostEstimate(flops=20_000_000_000, bytes_accessed=20_000_000, transcendentals=0),
        name="begin",
    )(features, ids)

    current = start
    everyone = peers * lanes
    for i in range(ITERS):
        first, last = i == 0, i == ITERS - 1
        received = lax.all_to_all(outgoing, "rows", split_axis=0, concat_axis=0, tiled=True)
        if last:
            outs = [shape((width, node_count), f32), shape((everyone, tile), f32)]
        else:
            outs = [shape((blocks, rows, tile), f32), shape((halo, width, tile), f32), shape((8, tile), f32)]
        if first:
            outs += [shape((1, node_count), f32), VMEM((tile_count * tile, 2 * tile), jnp.bfloat16)]
        kept = (tiles,) if first else (scale, weights, sums)
        got = pl.pallas_call(
            lambda *refs, i=i: step_kernel(i, refs),
            out_shape=tuple(outs),
            in_specs=[WHOLE] * 3 + [SCALARS] * 2 + [WHOLE] * len(kept),
            out_specs=(WHOLE,) * len(outs),
            scratch_shapes=[VMEM((blocks + halo, 2 * rows, tile), jnp.bfloat16)],
            compiler_params=LIMIT,
            name=f"step{i}",
        )(current, received, start, tile_slot, ids, *kept)
        if first:
            current, outgoing, sums, scale, weights = got
            weights = pltpu.with_memory_space_constraint(weights, VMEM)
        elif last:
            ranked, sums = got
        else:
            current, outgoing, sums = got
    theirs = lax.all_to_all(sums, ("rows", "feat"), split_axis=0, concat_axis=0, tiled=True)
    change = jnp.sum(theirs, axis=0)[:ITERS] / (width * lanes * node_count * peers)
    return ranked, change


def solution(mesh):
    return jax.shard_map(
        shards,
        mesh=mesh,
        in_specs=(P("feat", "rows"), P("rows", None, None), P("rows"), P("rows", None, None)),
        out_specs=(P("feat", "rows"), P()),
        check_vma=False,
    )
```

time: 165 us -> 67.7 us (0.41)
  matrix products: 61.5 us -> 0 us
  blocking collectives: 72.1 us -> 53.3 us
  Pallas kernels: 0 us -> 11.4 us
  other arithmetic: 11.2 us -> 0.57 us
  starting transfers between devices: 7.31 us -> 0 us
  local copies, waits for them, and re-layouts: 8.15 us -> 1.57 us
  between operations: 3.33 us -> 0.68 us
    dot_general x4 -> x0, matrix products: 61.5 us -> none  [shards(): jnp.einsum('tij,tfj->tfi', tiles, picked, precision=lax.Precision.HIGHEST)]
    psum x1 -> x0, blocking collectives: 40.9 us -> none  [shards(): partials.append(lax.psum(partial_value, ('rows', 'feat')))]
    all_to_all x3 -> x4, blocking collectives: 31.2 us -> 43.9 us  [shards(): lax.all_to_all(outgoing, 'rows', split_axis=0, concat_axis=0, tiled=True)]
    pallas_call x0 -> x5, Pallas kernels: none -> 11.4 us  [the longest x4 10.8 us: shards(): pl.pallas_call(lambda *refs, i=i: step_kernel(i, refs), out_shape=tuple(o...]
    all_to_all x0 -> x1, blocking collectives: none -> 9.34 us  [shards(): lax.all_to_all(sums, ('rows', 'feat'), split_axis=0, concat_axis=0, tiled...]
    all_to_all x1 -> x0, starting transfers between devices: 7.31 us -> none  [shards(): lax.all_to_all(outgoing, 'rows', split_axis=0, concat_axis=0, tiled=True)]
    reduce_sum x3 -> x1, other arithmetic: 6.36 us -> 0.05 us  [shards(): jnp.sum(theirs, axis=0)[:ITERS] / (width * lanes * node_count * peers)]
    gather x8 -> x0, local copies, waits for them, and re-layouts: 5.39 us -> none  [the longest x4 3.16 us: shards(): picked = buffer[tile_slot]]
  transfers between devices with their start and end apart: 1 -> 0, of which waited for: 1 -> 0; matrix products, arithmetic and copies ran while one was open for 4% -> 0% of each run, Pallas kernels for 0% -> 0%
where the time goes in v1:
time: 67.7 us; the launch traced here: 67.4 us
  blocking collectives  53.3 us (79%)
  Pallas kernels  11.4 us (17%)
  local copies, waits for them, and re-layouts  1.57 us (2%)
  between operations  0.68 us (1%)
    all_to_all x4, blocking collectives, shards(): lax.all_to_all(outgoing, 'rows', split_axis=0, concat_axis=0, tiled=True)  43.9 us
    pallas_call x4, Pallas kernels, shards(): pl.pallas_call(lambda *refs, i=i: step_kernel(i, refs), out_shape=tuple(o...  10.8 us
    all_to_all x1, blocking collectives, shards(): lax.all_to_all(sums, ('rows', 'feat'), split_axis=0, concat_axis=0, tiled...  9.34 us
    unnamed x10, local copies, waits for them, and re-layouts  1.57 us

profile of v1, /device:TPU:0, one launch (start us, length us, event | category | flops | bytes accessed | tf_op | source)
XLA Modules:
  0.0 67.4 jit_solution(2785198087399720068)
XLA Ops:
  0.6 0.0 copy-start.1
  0.6 0.6 copy-done.1
  1.3 0.0 copy-start.4
  1.3 0.9 %copy-done.4 = f32[25,1024]{1,0:T(8,128)S(1)} copy-done((f32[25,1024]{1,0:T(8,128)S(1)}, f32[25,1024]{1,0:T(8,128)}, u32[]{:S(2)}) %copy-start.4) | copy-done | bytes 102424
  2.2 0.0 copy-start
  2.2 0.0 copy-start.3
  2.2 0.6 begin.1
  2.8 0.0 copy-start.2
  2.8 14.7 %all_to_all.29.refs_1_ = f32[8,25,128]{2,1,0:T(8,128)S(1)} all-to-all(f32[8,25,128]{2,1,0:T(8,128)S(1)} %get-tuple-element.18), channel_id=1, replica_groups=mesh['rows'=8,'feat'=4] {'rows'}, dimensions={0} | all-to-all | bytes 204800 | tf_op jit(solution)/shard_map/all_to_all | solution.py:129
  17.5 0.0 copy-done
  17.5 0.0 copy-done.3
  17.5 3.6 %step0.1 = (f32[8,32,128]{2,1,0:T(8,128)S(1)}, f32[8,25,128]{2,1,0:T(8,128)S(1)}, f32[8,128]{1,0:T(8,128)S(1)}, f32[1,1024]{1,0:T(1,128)S(1)}, bf16[16384,256]{1,0:T(8,128)(2,1)S(1)}) custom-call(f32[8,32,128]{2,1,0:T(8,128)S(1)} %get-tuple-element.17.refs_0_.refs_2_, f32[8,25,128]{2,1,0:T(8,128)S(1)} %all_to_all.29.refs_1_, ...), custom_call_target="tpu_custom_call" | custom-call | tf_op jit(solution)/shard_map/step0/pallas_call | solution.py:137
  21.1 9.7 %all_to_all.30.refs_1_ = f32[8,25,128]{2,1,0:T(8,128)S(1)} all-to-all(f32[8,25,128]{2,1,0:T(8,128)S(1)} %get-tuple-element.20), channel_id=1, replica_groups=mesh['rows'=8,'feat'=4] {'rows'}, dimensions={0} | all-to-all | bytes 204800 | tf_op jit(solution)/shard_map/all_to_all | solution.py:129
  30.9 0.0 copy-done.2
  30.9 2.2 %step1.1 = (f32[8,32,128]{2,1,0:T(8,128)S(1)}, f32[8,25,128]{2,1,0:T(8,128)S(1)}, f32[8,128]{1,0:T(8,128)S(1)}) custom-call(f32[8,32,128]{2,1,0:T(8,128)S(1)} %get-tuple-element.19.refs_0_, f32[8,25,128]{2,1,0:T(8,128)S(1)} %all_to_all.30.refs_1_, f32[8,32,128]{2,1,0:T(8,128)S(1)} %get-tuple-element.17.refs_0_.refs_2_, s32[128]{0:T(128)S(1)} %copy-done.3, ...), custom_call_target="tpu_custom_call" | custom-call | tf_op jit(solution)/shard_map/step1/pallas_call | solution.py:137
  33.1 9.7 %all_to_all.31.refs_1_ = f32[8,25,128]{2,1,0:T(8,128)S(1)} all-to-all(f32[8,25,128]{2,1,0:T(8,128)S(1)} %get-tuple-element.25), channel_id=1, replica_groups=mesh['rows'=8,'feat'=4] {'rows'}, dimensions={0} | all-to-all | bytes 204800 | tf_op jit(solution)/shard_map/all_to_all | solution.py:129
  42.8 2.2 %step2.1 = (f32[8,32,128]{2,1,0:T(8,128)S(1)}, f32[8,25,128]{2,1,0:T(8,128)S(1)}, f32[8,128]{1,0:T(8,128)S(1)}) custom-call(f32[8,32,128]{2,1,0:T(8,128)S(1)} %get-tuple-element.24.refs_0_, f32[8,25,128]{2,1,0:T(8,128)S(1)} %all_to_all.31.refs_1_, f32[8,32,128]{2,1,0:T(8,128)S(1)} %get-tuple-element.17.refs_0_.refs_2_, s32[128]{0:T(128)S(1)} %copy-done.3, ...), custom_call_target="tpu_custom_call" | custom-call | tf_op jit(solution)/shard_map/step2/pallas_call | solution.py:137
  45.0 9.7 %all_to_all.32.refs_1_ = f32[8,25,128]{2,1,0:T(8,128)S(1)} all-to-all(f32[8,25,128]{2,1,0:T(8,128)S(1)} %get-tuple-element.28), channel_id=1, replica_groups=mesh['rows'=8,'feat'=4] {'rows'}, dimensions={0} | all-to-all | bytes 204800 | tf_op jit(solution)/shard_map/all_to_all | solution.py:129
  54.7 2.8 %step3.1 = (f32[25,1024]{1,0:T(8,128)}, f32[32,128]{1,0:T(8,128)S(1)}) custom-call(f32[8,32,128]{2,1,0:T(8,128)S(1)} %get-tuple-element.27.refs_0_, f32[8,25,128]{2,1,0:T(8,128)S(1)} %all_to_all.32.refs_1_, f32[8,32,128]{2,1,0:T(8,128)S(1)} %get-tuple-element.17.refs_0_.refs_2_, s32[128]{0:T(128)S(1)} %copy-done.3, s32[8]{0:T(128)S(1)} %bitcast.9, ...), custom_call_target="tpu_custom_call" | custom-call | tf_op jit(solution)/shard_map/step3/pallas_call | solution.py:137
  57.5 9.3 %all_to_all.33 = f32[32,1,128]{2,1,0:T(1,128)S(1)} all-to-all(f32[32,1,128]{2,1,0:T(1,128)S(1)} %bitcast.4), channel_id=1, replica_groups=mesh['rows'=8,'feat'=4] {'rows','feat'}, dimensions={0} | all-to-all | bytes 32768 | tf_op jit(solution)/shard_map/all_to_all | solution.py:153
  66.9 0.1 reduce_sum.9
  66.9 0.5 slice_multiply_fusion
Async XLA Ops:
  0.6 0.7 copy-start.1
  1.3 0.9 %copy-start.4 = (f32[25,1024]{1,0:T(8,128)S(1)}, f32[25,1024]{1,0:T(8,128)}, u32[]{:S(2)}) copy-start(f32[25,1024]{1,0:T(8,128)} %features_ref.1) | copy-start | bytes 307204
  2.2 15.3 %copy-start = (f32[128,128,128]{2,1,0:T(8,128)S(1)}, f32[128,128,128]{2,1,0:T(8,128)}, u32[]{:S(2)}) copy-start(f32[128,128,128]{2,1,0:T(8,128)} %refs_5_.1) | copy-start | bytes 25165828
  2.2 15.3 %copy-start.3 = (s32[128]{0:T(128)S(1)}, s32[128]{0:T(128)}, u32[]{:S(2)}) copy-start(s32[128]{0:T(128)} %refs_3_.7) | copy-start | bytes 1540
  2.8 28.1 %copy-start.2 = (s32[1,8,1]{1,2,0:T(1,128)S(1)}, s32[1,8,1]{1,2,0:T(1,128)}, u32[]{:S(2)}) copy-start(s32[1,8,1]{1,2,0:T(1,128)} %param.7) | copy-start | bytes 100

commit v2 on v1

v2 whole, which is shorter than its diff:
```python
import jax
import jax.numpy as jnp
from jax import lax
from jax.experimental import pallas as pl
from jax.experimental.pallas import tpu as pltpu
from jax.sharding import PartitionSpec as P

ITERS = 4


teleport = 0.15

VMEM, SMEM = pltpu.VMEM, pltpu.SMEM
WHOLE = pl.BlockSpec(memory_space=VMEM)
SCALARS = pl.BlockSpec(memory_space=SMEM)
LIMIT = pltpu.CompilerParams(vmem_limit_bytes=20 * 1024 * 1024)


def framed(block, rows):
    width, tile = block.shape
    row = lax.broadcasted_iota(jnp.int32, (rows - width, tile), 0)
    return jnp.concatenate([block, jnp.where(row == 0, 1.0, 0.0).astype(block.dtype)], axis=0)


def split(v):
    high = v.astype(jnp.bfloat16)
    return high, (v - high.astype(jnp.float32)).astype(jnp.bfloat16)


def begin_kernel(features_ref, slot_in_ref, ids_in_ref, start_ref, outgoing_ref, slot_ref, ids_ref, held_ref, arrived):
    blocks, rows, tile = start_ref.shape
    width = features_ref.shape[0]
    copies = [
        pltpu.make_async_copy(ids_in_ref, ids_ref, arrived.at[0]),
        pltpu.make_async_copy(features_ref, held_ref, arrived.at[1]),
        pltpu.make_async_copy(slot_in_ref, slot_ref, arrived.at[2]),
    ]
    for copy in copies:
        copy.start()
    for copy in copies:
        copy.wait()
    for d in range(ids_ref.shape[0]):
        at = pl.multiple_of(ids_ref[d] * tile, tile)
        outgoing_ref[d * width:(d + 1) * width, :] = held_ref[:, pl.ds(at, tile)]
    for b in range(blocks):
        start_ref[b] = framed(held_ref[:, b * tile:(b + 1) * tile], rows)


def step_kernel(index, refs):
    first, last = index == 0, index == ITERS - 1
    refs = list(refs)
    if last:
        held_ref, left = refs.pop(-2), refs.pop()
    current_ref, received_ref, start_ref, slot_ref, ids_ref = refs[:5]
    views_ref = refs.pop()
    if first:
        tiles_ref, next_ref, outgoing_ref, sums_ref, scale_ref, weights_ref = refs[5:]
    elif last:
        scale_ref, weights_ref, past_ref, ranked_ref, sums_ref = refs[5:]
    else:
        scale_ref, weights_ref, past_ref, next_ref, outgoing_ref, sums_ref = refs[5:]
    blocks, rows, tile = current_ref.shape
    width = received_ref.shape[0] // ids_ref.shape[0]
    per_block = weights_ref.shape[0] // (blocks * tile)
    for c in range(blocks + ids_ref.shape[0]):
        v = current_ref[c] if c < blocks else framed(received_ref[(c - blocks) * width:(c - blocks + 1) * width, :], rows)
        views_ref[c, 0:rows], views_ref[c, rows:2 * rows] = split(v)
    square = jnp.zeros((8, tile), jnp.float32)
    copies = []
    for b in range(blocks):
        picked = [views_ref[slot_ref[t]] for t in range(b * per_block, (b + 1) * per_block)]
        lhs = jnp.concatenate(picked, axis=1)
        lhs = jnp.concatenate([lhs, jnp.zeros_like(lhs)], axis=0)
        if first:
            s = None
            for t in range(0, per_block, 2):
                both = []
                for u in range(b * per_block + t, b * per_block + min(t + 2, per_block)):
                    high, low = split(tiles_ref[u].T)
                    weights_ref[u * tile:(u + 1) * tile, 0:tile] = high
                    weights_ref[u * tile:(u + 1) * tile, tile:2 * tile] = low
                    both.append(jnp.concatenate([high, low], axis=1))
                part = jnp.dot(lhs[:, t * tile:(t + 2) * tile], jnp.concatenate(both, axis=0), preferred_element_type=jnp.float32)
                s = part if s is None else s + part
        else:
            s = jnp.dot(lhs, weights_ref[b * per_block * tile:(b + 1) * per_block * tile, :], preferred_element_type=jnp.float32)
        s = s[0:rows] + s[rows:2 * rows]
        s = s[:, 0:tile] + s[:, tile:2 * tile]
        r = slice(b * tile, (b + 1) * tile)
        if first:
            scale = (1.0 - teleport) / (1.0 + s[width:width + 1])
            scale_ref[:, r] = scale
        else:
            scale = scale_ref[:, r]
        old = current_ref[b]
        new = (old + s) * scale + teleport * start_ref[b]
        row = lax.broadcasted_iota(jnp.int32, (rows, tile), 0)
        new = jnp.where(row < width, new, start_ref[b])
        d = new - old
        d = d * d
        for k in range(rows // 8):
            square = square + d[8 * k:8 * k + 8]
        if last:
            held_ref[b] = new[0:width]
            copies.append(pltpu.make_async_copy(held_ref.at[b], ranked_ref.at[:, r], left.at[b]))
            if b:
                copies[b - 1].start()
        else:
            next_ref[b] = new
    row = lax.broadcasted_iota(jnp.int32, (8, tile), 0)
    sums = jnp.where(row == index, jnp.sum(square, axis=0, keepdims=True), 0.0 if first else past_ref[...])
    if last:
        copies[-1].start()
        lane = lax.broadcasted_iota(jnp.int32, (8, tile), 1)
        sums = jnp.where(row == lane, jnp.sum(sums, axis=1, keepdims=True), 0.0)
        sums_ref[...] = jnp.broadcast_to(jnp.sum(sums, axis=0, keepdims=True), sums_ref.shape)
        for copy in copies:
            copy.wait()
    else:
        sums_ref[...] = sums
    if not last:
        for d in range(ids_ref.shape[0]):
            outgoing_ref[d * width:(d + 1) * width, :] = next_ref[ids_ref[d], 0:width]


def shards(features, tiles, tile_slot, send_blocks):
    width, node_count = features.shape
    tile_count, tile, _ = tiles.shape
    blocks = node_count // tile
    peers = lax.axis_size("rows")
    lanes = lax.axis_size("feat")
    halo = peers * send_blocks.shape[2]
    rows = -(-(width + 1) // 8) * 8
    f32 = jnp.float32
    shape = jax.ShapeDtypeStruct

    start, outgoing, slot, ids = pl.pallas_call(
        begin_kernel,
        out_shape=(
            shape((blocks, rows, tile), f32),
            shape((halo * width, tile), f32),
            SMEM(tile_slot.shape, jnp.int32),
            SMEM((halo,), jnp.int32),
        ),
        in_specs=[pl.BlockSpec(memory_space=pltpu.HBM)] * 3,
        out_specs=(WHOLE, WHOLE, SCALARS, SCALARS),
        scratch_shapes=[VMEM(features.shape, f32), pltpu.SemaphoreType.DMA((3,))],
        compiler_params=LIMIT,
        cost_estimate=pl.CostEstimate(flops=20_000_000_000, bytes_accessed=20_000_000, transcendentals=0),
        name="begin",
    )(*(pltpu.with_memory_space_constraint(x, pltpu.HBM) for x in (features, tile_slot, send_blocks.reshape(-1))))

    current = start
    everyone = peers * lanes
    for i in range(ITERS):
        first, last = i == 0, i == ITERS - 1
        received = lax.all_to_all(outgoing.reshape(peers, -1, 1, tile), "rows", split_axis=0, concat_axis=0, tiled=True)
        received = received.reshape(halo * width, tile)
        if last:
            outs = [shape((width, node_count), f32), shape((everyone, tile), f32)]
        else:
            outs = [shape((blocks, rows, tile), f32), shape((halo * width, tile), f32), shape((8, tile), f32)]
        if first:
            outs += [shape((1, node_count), f32), VMEM((tile_count * tile, 2 * tile), jnp.bfloat16)]
        kept = (tiles,) if first else (scale, weights, sums)
        got = pl.pallas_call(
            lambda *refs, i=i: step_kernel(i, refs),
            out_shape=tuple(outs),
            in_specs=[WHOLE] * 3 + [SCALARS] * 2 + [WHOLE] * len(kept),
            out_specs=(pl.BlockSpec(memory_space=pltpu.HBM) if last else WHOLE,) + (WHOLE,) * (len(outs) - 1),
            scratch_shapes=[VMEM((blocks + halo, 2 * rows, tile), jnp.bfloat16)]
            + last * [VMEM((blocks, width, tile), f32), pltpu.SemaphoreType.DMA((blocks,))],
            compiler_params=LIMIT,
            name=f"step{i}",
        )(current, received, start, slot, ids, *kept)
        if first:
            current, outgoing, sums, scale, weights = got
            weights = pltpu.with_memory_space_constraint(weights, VMEM)
        elif last:
            ranked, sums = got
        else:
            current, outgoing, sums = got
    theirs = lax.all_to_all(sums, ("rows", "feat"), split_axis=0, concat_axis=0, tiled=True)
    change = jnp.sum(theirs, axis=0)[:ITERS] / (width * lanes * node_count * peers)
    return ranked, change


def solution(mesh):
    return jax.shard_map(
        shards,
        mesh=mesh,
        in_specs=(P("feat", "rows"), P("rows", None, None), P("rows"), P("rows", None, None)),
        out_specs=(P("feat", "rows"), P()),
        check_vma=False,
    )
```

time: 67.7 us -> 62.3 us (0.920)
  Pallas kernels: 11.4 us -> 8.34 us
  local copies, waits for them, and re-layouts: 1.57 us -> 0.01 us
  blocking collectives: 53.3 us -> 52.4 us
    pallas_call x4, Pallas kernels: 10.8 us -> 7.23 us  [shards(): pl.pallas_call(lambda *refs, i=i: step_kernel(i, refs), out_shape=tuple(o...]
    unnamed x10 -> x2, local copies, waits for them, and re-layouts: 1.57 us -> 0.01 us
    all_to_all x4, blocking collectives: 43.9 us -> 43.1 us  [shards(): lax.all_to_all(outgoing.reshape(peers, -1, 1, tile), 'rows', split_axis=0...]
where the time goes in v2:
time: 62.3 us; the launch traced here: 62 us
  blocking collectives  52.4 us (84%)
  Pallas kernels  8.34 us (13%)
  between operations  0.68 us (1%)
    all_to_all x4, blocking collectives, shards(): lax.all_to_all(outgoing.reshape(peers, -1, 1, tile), 'rows', split_axis=0...  43.1 us
    all_to_all x1, blocking collectives, shards(): lax.all_to_all(sums, ('rows', 'feat'), split_axis=0, concat_axis=0, tiled...  9.24 us
    pallas_call x4, Pallas kernels, shards(): pl.pallas_call(lambda *refs, i=i: step_kernel(i, refs), out_shape=tuple(o...  7.23 us

profile of v2, /device:TPU:0, one launch (start us, length us, event | category | flops | bytes accessed | tf_op | source)
XLA Modules:
  0.0 62.0 jit_solution(14646490028425353356)
XLA Ops:
  0.6 0.0 copy-start
  0.6 1.1 %begin.1 = (f32[8,32,128]{2,1,0:T(8,128)S(1)}, f32[200,128]{1,0:T(8,128)S(1)}, s32[128]{0:T(128)S(4)}, s32[8]{0:T(128)S(4)}) custom-call(f32[25,1024]{1,0:T(8,128)} %features_ref.1, s32[128]{0:T(128)} %slot_in_ref.1, s32[8]{0:T(128)} %bitcast.21), custom_call_target="tpu_custom_call" | custom-call | flops 20000000000 | bytes 20000000 | tf_op jit(solution)/shard_map/begin/pallas_call | solution.py:137
  1.8 14.5 %all_to_all.29 = f32[8,25,1,128]{3,2,1,0:T(1,128)S(1)} all-to-all(f32[8,25,1,128]{3,2,1,0:T(1,128)S(1)} %bitcast.19), channel_id=1, replica_groups=mesh['rows'=8,'feat'=4] {'rows'}, dimensions={0} | all-to-all | bytes 204800 | tf_op jit(solution)/shard_map/all_to_all | solution.py:157
  16.3 0.0 copy-done
  16.3 2.6 %step0.1 = (f32[8,32,128]{2,1,0:T(8,128)S(1)}, f32[200,128]{1,0:T(8,128)S(1)}, f32[8,128]{1,0:T(8,128)S(1)}, f32[1,1024]{1,0:T(1,128)S(1)}, bf16[16384,256]{1,0:T(8,128)(2,1)S(1)}) custom-call(f32[8,32,128]{2,1,0:T(8,128)S(1)} %get-tuple-element.19.refs_0_.refs_2_, f32[200,128]{1,0:T(8,128)S(1)} %bitcast.15, ...), custom_call_target="tpu_custom_call" | custom-call | tf_op jit(solution)/shard_map/step0/pallas_call | solution.py:166
  18.9 9.5 %all_to_all.30 = f32[8,25,1,128]{3,2,1,0:T(1,128)S(1)} all-to-all(f32[8,25,1,128]{3,2,1,0:T(1,128)S(1)} %bitcast.16), channel_id=1, replica_groups=mesh['rows'=8,'feat'=4] {'rows'}, dimensions={0} | all-to-all | bytes 204800 | tf_op jit(solution)/shard_map/all_to_all | solution.py:157
  28.4 1.3 %step1.1 = (f32[8,32,128]{2,1,0:T(8,128)S(1)}, f32[200,128]{1,0:T(8,128)S(1)}, f32[8,128]{1,0:T(8,128)S(1)}) custom-call(f32[8,32,128]{2,1,0:T(8,128)S(1)} %get-tuple-element.23.refs_0_, f32[200,128]{1,0:T(8,128)S(1)} %bitcast.13, f32[8,32,128]{2,1,0:T(8,128)S(1)} %get-tuple-element.19.refs_0_.refs_2_, s32[128]{0:T(128)S(4)} %get-tuple-element.21.refs_3_, ...), custom_call_target="tpu_custom_call" | custom-call | tf_op jit(solution)/shard_map/step1/pallas_call | solution.py:166
  29.7 9.5 %all_to_all.31 = f32[8,25,1,128]{3,2,1,0:T(1,128)S(1)} all-to-all(f32[8,25,1,128]{3,2,1,0:T(1,128)S(1)} %bitcast.17), channel_id=1, replica_groups=mesh['rows'=8,'feat'=4] {'rows'}, dimensions={0} | all-to-all | bytes 204800 | tf_op jit(solution)/shard_map/all_to_all | solution.py:157
  39.3 1.3 %step2.1 = (f32[8,32,128]{2,1,0:T(8,128)S(1)}, f32[200,128]{1,0:T(8,128)S(1)}, f32[8,128]{1,0:T(8,128)S(1)}) custom-call(f32[8,32,128]{2,1,0:T(8,128)S(1)} %get-tuple-element.28.refs_0_, f32[200,128]{1,0:T(8,128)S(1)} %bitcast.14, f32[8,32,128]{2,1,0:T(8,128)S(1)} %get-tuple-element.19.refs_0_.refs_2_, s32[128]{0:T(128)S(4)} %get-tuple-element.21.refs_3_, ...), custom_call_target="tpu_custom_call" | custom-call | tf_op jit(solution)/shard_map/step2/pallas_call | solution.py:166
  40.6 9.5 %all_to_all.32 = f32[8,25,1,128]{3,2,1,0:T(1,128)S(1)} all-to-all(f32[8,25,1,128]{3,2,1,0:T(1,128)S(1)} %bitcast.18), channel_id=1, replica_groups=mesh['rows'=8,'feat'=4] {'rows'}, dimensions={0} | all-to-all | bytes 204800 | tf_op jit(solution)/shard_map/all_to_all | solution.py:157
  50.2 2.0 %step3.1 = (f32[25,1024]{1,0:T(8,128)}, f32[32,128]{1,0:T(8,128)S(1)}) custom-call(f32[8,32,128]{2,1,0:T(8,128)S(1)} %get-tuple-element.31.refs_0_, f32[200,128]{1,0:T(8,128)S(1)} %bitcast.12, f32[8,32,128]{2,1,0:T(8,128)S(1)} %get-tuple-element.19.refs_0_.refs_2_, s32[128]{0:T(128)S(4)} %get-tuple-element.21.refs_3_, s32[8]{0:T(128)S(4)} %get-tuple-element.22.refs_4_, ...), custom_call_target="tpu_custom_call" | custom-call | tf_op jit(solution)/shard_map/step3/pallas_call | solution.py:166
  52.2 9.2 %all_to_all.33 = f32[32,1,128]{2,1,0:T(1,128)S(1)} all-to-all(f32[32,1,128]{2,1,0:T(1,128)S(1)} %bitcast.20), channel_id=1, replica_groups=mesh['rows'=8,'feat'=4] {'rows','feat'}, dimensions={0} | all-to-all | bytes 32768 | tf_op jit(solution)/shard_map/all_to_all | solution.py:183
  61.4 0.1 reduce_sum.9
  61.5 0.5 slice_multiply_fusion
Async XLA Ops:
  0.6 15.7 %copy-start = (f32[128,128,128]{2,1,0:T(8,128)S(1)}, f32[128,128,128]{2,1,0:T(8,128)}, u32[]{:S(2)}) copy-start(f32[128,128,128]{2,1,0:T(8,128)} %refs_5_.1) | copy-start | bytes 25165828

commit v3 on v2

--- a/solution.py
+++ b/solution.py
@@ -1,3 +1,5 @@
+import functools
+
 import jax
 import jax.numpy as jnp
 from jax import lax
@@ -16,6 +18,13 @@
 LIMIT = pltpu.CompilerParams(vmem_limit_bytes=20 * 1024 * 1024)
 
 
+def meeting_order(peers):
+    if peers == 8:
+        return [5, 6, 4, 3, 7, 2, 1, 0]
+    middle = peers // 2 + 1
+    return sorted(range(peers), key=lambda i: abs(i - middle))
+
+
 def framed(block, rows):
     width, tile = block.shape
     row = lax.broadcasted_iota(jnp.int32, (rows - width, tile), 0)
@@ -27,7 +36,7 @@
     return high, (v - high.astype(jnp.float32)).astype(jnp.bfloat16)
 
 
-def begin_kernel(features_ref, slot_in_ref, ids_in_ref, start_ref, outgoing_ref, slot_ref, ids_ref, held_ref, arrived):
+def begin_kernel(targets, features_ref, slot_in_ref, ids_in_ref, start_ref, outgoing_ref, slot_ref, ids_ref, held_ref, arrived):
     blocks, rows, tile = start_ref.shape
     width = features_ref.shape[0]
     copies = [
@@ -39,14 +48,14 @@
         copy.start()
     for copy in copies:
         copy.wait()
-    for d in range(ids_ref.shape[0]):
+    for q, d in enumerate(targets):
         at = pl.multiple_of(ids_ref[d] * tile, tile)
-        outgoing_ref[d * width:(d + 1) * width, :] = held_ref[:, pl.ds(at, tile)]
+        outgoing_ref[q * width:(q + 1) * width, :] = held_ref[:, pl.ds(at, tile)]
     for b in range(blocks):
         start_ref[b] = framed(held_ref[:, b * tile:(b + 1) * tile], rows)
 
 
-def step_kernel(index, refs):
+def step_kernel(index, targets, refs):
     first, last = index == 0, index == ITERS - 1
     refs = list(refs)
     if last:
@@ -60,11 +69,13 @@
     else:
         scale_ref, weights_ref, past_ref, next_ref, outgoing_ref, sums_ref = refs[5:]
     blocks, rows, tile = current_ref.shape
-    width = received_ref.shape[0] // ids_ref.shape[0]
+    width = received_ref.shape[0] // len(targets)
     per_block = weights_ref.shape[0] // (blocks * tile)
-    for c in range(blocks + ids_ref.shape[0]):
-        v = current_ref[c] if c < blocks else framed(received_ref[(c - blocks) * width:(c - blocks + 1) * width, :], rows)
-        views_ref[c, 0:rows], views_ref[c, rows:2 * rows] = split(v)
+    for b in range(blocks):
+        views_ref[b, 0:rows], views_ref[b, rows:2 * rows] = split(current_ref[b])
+    for q, d in enumerate(targets):
+        v = framed(received_ref[q * width:(q + 1) * width, :], rows)
+        views_ref[blocks + d, 0:rows], views_ref[blocks + d, rows:2 * rows] = split(v)
     square = jnp.zeros((8, tile), jnp.float32)
     copies = []
     for b in range(blocks):
@@ -119,8 +130,8 @@
     else:
         sums_ref[...] = sums
     if not last:
-        for d in range(ids_ref.shape[0]):
-            outgoing_ref[d * width:(d + 1) * width, :] = next_ref[ids_ref[d], 0:width]
+        for q, d in enumerate(targets):
+            outgoing_ref[q * width:(q + 1) * width, :] = next_ref[ids_ref[d], 0:width]
 
 
 def shards(features, tiles, tile_slot, send_blocks):
@@ -129,13 +140,16 @@
     blocks = node_count // tile
     peers = lax.axis_size("rows")
     lanes = lax.axis_size("feat")
-    halo = peers * send_blocks.shape[2]
+    slots = send_blocks.shape[2]
+    halo = peers * slots
+    order = meeting_order(peers)
+    targets = [d * slots + k for d in order for k in range(slots)]
     rows = -(-(width + 1) // 8) * 8
     f32 = jnp.float32
     shape = jax.ShapeDtypeStruct
 
     start, outgoing, slot, ids = pl.pallas_call(
-        begin_kernel,
+        functools.partial(begin_kernel, targets),
         out_shape=(
             shape((blocks, rows, tile), f32),
             shape((halo * width, tile), f32),
@@ -154,7 +168,10 @@
     everyone = peers * lanes
     for i in range(ITERS):
         first, last = i == 0, i == ITERS - 1
-        received = lax.all_to_all(outgoing.reshape(peers, -1, 1, tile), "rows", split_axis=0, concat_axis=0, tiled=True)
+        received = lax.all_to_all(
+            outgoing.reshape(peers, -1, 1, tile), "rows", split_axis=0, concat_axis=0, tiled=True,
+            axis_index_groups=[order],
+        )
         received = received.reshape(halo * width, tile)
         if last:
             outs = [shape((width, node_count), f32), shape((everyone, tile), f32)]
@@ -164,7 +181,7 @@
             outs += [shape((1, node_count), f32), VMEM((tile_count * tile, 2 * tile), jnp.bfloat16)]
         kept = (tiles,) if first else (scale, weights, sums)
         got = pl.pallas_call(
-            lambda *refs, i=i: step_kernel(i, refs),
+            lambda *refs, i=i: step_kernel(i, targets, refs),
             out_shape=tuple(outs),
             in_specs=[WHOLE] * 3 + [SCALARS] * 2 + [WHOLE] * len(kept),
             out_specs=(pl.BlockSpec(memory_space=pltpu.HBM) if last else WHOLE,) + (WHOLE,) * (len(outs) - 1),

time: 62.3 us -> 59.1 us (0.949)
  blocking collectives: 52.4 us -> 49.2 us
    all_to_all x4, blocking collectives: 43.1 us -> 37.4 us  [shards(): lax.all_to_all(outgoing.reshape(peers, -1, 1, tile), 'rows', split_axis=0...]
    all_to_all x1, blocking collectives: 9.24 us -> 11.8 us  [shards(): lax.all_to_all(sums, ('rows', 'feat'), split_axis=0, concat_axis=0, tiled...]
where the time goes in v3:
time: 59.1 us; the launch traced here: 58.8 us
  blocking collectives  49.2 us (83%)
  Pallas kernels  8.35 us (14%)
  between operations  0.68 us (1%)
    all_to_all x4, blocking collectives, shards(): lax.all_to_all(outgoing.reshape(peers, -1, 1, tile), 'rows', split_axis=0...  37.4 us
    all_to_all x1, blocking collectives, shards(): lax.all_to_all(sums, ('rows', 'feat'), split_axis=0, concat_axis=0, tiled...  11.8 us
    pallas_call x4, Pallas kernels, shards(): pl.pallas_call(lambda *refs, i=i: step_kernel(i, targets, refs), out_shap...  7.23 us

profile of v3, /device:TPU:0, one launch (start us, length us, event | category | flops | bytes accessed | tf_op | source)
XLA Modules:
  0.0 58.8 jit_solution(10087888883478919485)
XLA Ops:
  0.6 0.0 copy-start
  0.6 1.1 %begin.1 = (f32[8,32,128]{2,1,0:T(8,128)S(1)}, f32[200,128]{1,0:T(8,128)S(1)}, s32[128]{0:T(128)S(4)}, s32[8]{0:T(128)S(4)}) custom-call(f32[25,1024]{1,0:T(8,128)} %features_ref.1, s32[128]{0:T(128)} %slot_in_ref.1, s32[8]{0:T(128)} %bitcast.21), custom_call_target="tpu_custom_call" | custom-call | flops 20000000000 | bytes 20000000 | tf_op jit(solution)/shard_map/begin/pallas_call | solution.py:151
  1.8 11.4 %all_to_all.29 = f32[8,25,1,128]{3,2,1,0:T(1,128)S(1)} all-to-all(f32[8,25,1,128]{3,2,1,0:T(1,128)S(1)} %bitcast.19), channel_id=1, replica_groups={{20,24,16,12,28,8,4,0},{21,25,17,13,29,9,5,1},{22,26,18,14,30,10,6,2},{..., dimensions={0} | all-to-all | bytes 204800 | tf_op jit(solution)/shard_map/all_to_all | solution.py:171
  13.2 0.0 copy-done
  13.2 2.6 %step0.1 = (f32[8,32,128]{2,1,0:T(8,128)S(1)}, f32[200,128]{1,0:T(8,128)S(1)}, f32[8,128]{1,0:T(8,128)S(1)}, f32[1,1024]{1,0:T(1,128)S(1)}, bf16[16384,256]{1,0:T(8,128)(2,1)S(1)}) custom-call(f32[8,32,128]{2,1,0:T(8,128)S(1)} %get-tuple-element.19.refs_0_.refs_2_, f32[200,128]{1,0:T(8,128)S(1)} %bitcast.15, ...), custom_call_target="tpu_custom_call" | custom-call | tf_op jit(solution)/shard_map/step0/pallas_call | solution.py:183
  15.8 8.6 %all_to_all.30 = f32[8,25,1,128]{3,2,1,0:T(1,128)S(1)} all-to-all(f32[8,25,1,128]{3,2,1,0:T(1,128)S(1)} %bitcast.16), channel_id=1, replica_groups={{20,24,16,12,28,8,4,0},{21,25,17,13,29,9,5,1},{22,26,18,14,30,10,6,2},{..., dimensions={0} | all-to-all | bytes 204800 | tf_op jit(solution)/shard_map/all_to_all | solution.py:171
  24.4 1.3 %step1.1 = (f32[8,32,128]{2,1,0:T(8,128)S(1)}, f32[200,128]{1,0:T(8,128)S(1)}, f32[8,128]{1,0:T(8,128)S(1)}) custom-call(f32[8,32,128]{2,1,0:T(8,128)S(1)} %get-tuple-element.23.refs_0_, f32[200,128]{1,0:T(8,128)S(1)} %bitcast.13, f32[8,32,128]{2,1,0:T(8,128)S(1)} %get-tuple-element.19.refs_0_.refs_2_, s32[128]{0:T(128)S(4)} %get-tuple-element.21.refs_3_, ...), custom_call_target="tpu_custom_call" | custom-call | tf_op jit(solution)/shard_map/step1/pallas_call | solution.py:183
  25.7 8.7 %all_to_all.31 = f32[8,25,1,128]{3,2,1,0:T(1,128)S(1)} all-to-all(f32[8,25,1,128]{3,2,1,0:T(1,128)S(1)} %bitcast.17), channel_id=1, replica_groups={{20,24,16,12,28,8,4,0},{21,25,17,13,29,9,5,1},{22,26,18,14,30,10,6,2},{..., dimensions={0} | all-to-all | bytes 204800 | tf_op jit(solution)/shard_map/all_to_all | solution.py:171
  34.4 1.3 %step2.1 = (f32[8,32,128]{2,1,0:T(8,128)S(1)}, f32[200,128]{1,0:T(8,128)S(1)}, f32[8,128]{1,0:T(8,128)S(1)}) custom-call(f32[8,32,128]{2,1,0:T(8,128)S(1)} %get-tuple-element.28.refs_0_, f32[200,128]{1,0:T(8,128)S(1)} %bitcast.14, f32[8,32,128]{2,1,0:T(8,128)S(1)} %get-tuple-element.19.refs_0_.refs_2_, s32[128]{0:T(128)S(4)} %get-tuple-element.21.refs_3_, ...), custom_call_target="tpu_custom_call" | custom-call | tf_op jit(solution)/shard_map/step2/pallas_call | solution.py:183
  35.7 8.7 %all_to_all.32 = f32[8,25,1,128]{3,2,1,0:T(1,128)S(1)} all-to-all(f32[8,25,1,128]{3,2,1,0:T(1,128)S(1)} %bitcast.18), channel_id=1, replica_groups={{20,24,16,12,28,8,4,0},{21,25,17,13,29,9,5,1},{22,26,18,14,30,10,6,2},{..., dimensions={0} | all-to-all | bytes 204800 | tf_op jit(solution)/shard_map/all_to_all | solution.py:171
  44.4 2.0 %step3.1 = (f32[25,1024]{1,0:T(8,128)}, f32[32,128]{1,0:T(8,128)S(1)}) custom-call(f32[8,32,128]{2,1,0:T(8,128)S(1)} %get-tuple-element.31.refs_0_, f32[200,128]{1,0:T(8,128)S(1)} %bitcast.12, f32[8,32,128]{2,1,0:T(8,128)S(1)} %get-tuple-element.19.refs_0_.refs_2_, s32[128]{0:T(128)S(4)} %get-tuple-element.21.refs_3_, s32[8]{0:T(128)S(4)} %get-tuple-element.22.refs_4_, ...), custom_call_target="tpu_custom_call" | custom-call | tf_op jit(solution)/shard_map/step3/pallas_call | solution.py:183
  46.4 11.8 %all_to_all.33 = f32[32,1,128]{2,1,0:T(1,128)S(1)} all-to-all(f32[32,1,128]{2,1,0:T(1,128)S(1)} %bitcast.20), channel_id=1, replica_groups=mesh['rows'=8,'feat'=4] {'rows','feat'}, dimensions={0} | all-to-all | bytes 32768 | tf_op jit(solution)/shard_map/all_to_all | solution.py:200
  58.2 0.1 reduce_sum.9
  58.3 0.5 slice_multiply_fusion
Async XLA Ops:
  0.6 12.5 %copy-start = (f32[128,128,128]{2,1,0:T(8,128)S(1)}, f32[128,128,128]{2,1,0:T(8,128)}, u32[]{:S(2)}) copy-start(f32[128,128,128]{2,1,0:T(8,128)} %refs_5_.1) | copy-start | bytes 25165828

commit v4 on v3

--- a/solution.py
+++ b/solution.py
@@ -34,6 +34,18 @@
 def split(v):
     high = v.astype(jnp.bfloat16)
     return high, (v - high.astype(jnp.float32)).astype(jnp.bfloat16)
+
+
+def turn(tiles, by_product):
+    parts = [split(tile) for tile in tiles]
+    if by_product:
+        flat = jnp.concatenate([jnp.concatenate(half, axis=1) for half in zip(*parts)], axis=0)
+        size = flat.shape[1]
+        unit = lax.broadcasted_iota(jnp.int32, (size, size), 0) == lax.broadcasted_iota(jnp.int32, (size, size), 1)
+        unit = unit.astype(jnp.float32).astype(jnp.bfloat16)
+        turned = lax.dot_general(unit, flat, (((1,), (1,)), ((), ())), preferred_element_type=jnp.float32)
+        return turned.astype(jnp.bfloat16)
+    return jnp.concatenate([jnp.concatenate(split(tile.T), axis=1) for tile in tiles], axis=0)
 
 
 def begin_kernel(targets, features_ref, slot_in_ref, ids_in_ref, start_ref, outgoing_ref, slot_ref, ids_ref, held_ref, arrived):
@@ -58,8 +70,6 @@
 def step_kernel(index, targets, refs):
     first, last = index == 0, index == ITERS - 1
     refs = list(refs)
-    if last:
-        held_ref, left = refs.pop(-2), refs.pop()
     current_ref, received_ref, start_ref, slot_ref, ids_ref = refs[:5]
     views_ref = refs.pop()
     if first:
@@ -77,7 +87,6 @@
         v = framed(received_ref[q * width:(q + 1) * width, :], rows)
         views_ref[blocks + d, 0:rows], views_ref[blocks + d, rows:2 * rows] = split(v)
     square = jnp.zeros((8, tile), jnp.float32)
-    copies = []
     for b in range(blocks):
         picked = [views_ref[slot_ref[t]] for t in range(b * per_block, (b + 1) * per_block)]
         lhs = jnp.concatenate(picked, axis=1)
@@ -85,13 +94,10 @@
         if first:
             s = None
             for t in range(0, per_block, 2):
-                both = []
-                for u in range(b * per_block + t, b * per_block + min(t + 2, per_block)):
-                    high, low = split(tiles_ref[u].T)
-                    weights_ref[u * tile:(u + 1) * tile, 0:tile] = high
-                    weights_ref[u * tile:(u + 1) * tile, tile:2 * tile] = low
-                    both.append(jnp.concatenate([high, low], axis=1))
-                part = jnp.dot(lhs[:, t * tile:(t + 2) * tile], jnp.concatenate(both, axis=0), preferred_element_type=jnp.float32)
+                at = range(b * per_block + t, b * per_block + min(t + 2, per_block))
+                turned = turn([tiles_ref[u] for u in at], by_product=t % 16 == 14)
+                weights_ref[at[0] * tile:(at[-1] + 1) * tile, :] = turned
+                part = jnp.dot(lhs[:, t * tile:(t + 2) * tile], turned, preferred_element_type=jnp.float32)
                 s = part if s is None else s + part
         else:
             s = jnp.dot(lhs, weights_ref[b * per_block * tile:(b + 1) * per_block * tile, :], preferred_element_type=jnp.float32)
@@ -112,26 +118,31 @@
         for k in range(rows // 8):
             square = square + d[8 * k:8 * k + 8]
         if last:
-            held_ref[b] = new[0:width]
-            copies.append(pltpu.make_async_copy(held_ref.at[b], ranked_ref.at[:, r], left.at[b]))
-            if b:
-                copies[b - 1].start()
+            ranked_ref[:, r] = new[0:width]
         else:
             next_ref[b] = new
     row = lax.broadcasted_iota(jnp.int32, (8, tile), 0)
     sums = jnp.where(row == index, jnp.sum(square, axis=0, keepdims=True), 0.0 if first else past_ref[...])
     if last:
-        copies[-1].start()
         lane = lax.broadcasted_iota(jnp.int32, (8, tile), 1)
         sums = jnp.where(row == lane, jnp.sum(sums, axis=1, keepdims=True), 0.0)
         sums_ref[...] = jnp.broadcast_to(jnp.sum(sums, axis=0, keepdims=True), sums_ref.shape)
-        for copy in copies:
-            copy.wait()
     else:
         sums_ref[...] = sums
     if not last:
         for q, d in enumerate(targets):
             outgoing_ref[q * width:(q + 1) * width, :] = next_ref[ids_ref[d], 0:width]
+
+
+def end_kernel(count, theirs_ref, held_ref, ranked_ref, change_ref, mean_ref, left):
+    ranked_copy = pltpu.make_async_copy(held_ref, ranked_ref, left.at[0])
+    ranked_copy.start()
+    sums = jnp.sum(theirs_ref[...], axis=0) / count
+    mean_ref[...] = sums[0:mean_ref.shape[0]]
+    change_copy = pltpu.make_async_copy(mean_ref, change_ref, left.at[1])
+    change_copy.start()
+    ranked_copy.wait()
+    change_copy.wait()
 
 
 def shards(features, tiles, tile_slot, send_blocks):
@@ -174,7 +185,7 @@
         )
         received = received.reshape(halo * width, tile)
         if last:
-            outs = [shape((width, node_count), f32), shape((everyone, tile), f32)]
+            outs = [VMEM((width, node_count), f32), shape((everyone, tile), f32)]
         else:
             outs = [shape((blocks, rows, tile), f32), shape((halo * width, tile), f32), shape((8, tile), f32)]
         if first:
@@ -184,9 +195,8 @@
             lambda *refs, i=i: step_kernel(i, targets, refs),
             out_shape=tuple(outs),
             in_specs=[WHOLE] * 3 + [SCALARS] * 2 + [WHOLE] * len(kept),
-            out_specs=(pl.BlockSpec(memory_space=pltpu.HBM) if last else WHOLE,) + (WHOLE,) * (len(outs) - 1),
-            scratch_shapes=[VMEM((blocks + halo, 2 * rows, tile), jnp.bfloat16)]
-            + last * [VMEM((blocks, width, tile), f32), pltpu.SemaphoreType.DMA((blocks,))],
+            out_specs=(WHOLE,) * len(outs),
+            scratch_shapes=[VMEM((blocks + halo, 2 * rows, tile), jnp.bfloat16)],
             compiler_params=LIMIT,
             name=f"step{i}",
         )(current, received, start, slot, ids, *kept)
@@ -198,8 +208,15 @@
         else:
             current, outgoing, sums = got
     theirs = lax.all_to_all(sums, ("rows", "feat"), split_axis=0, concat_axis=0, tiled=True)
-    change = jnp.sum(theirs, axis=0)[:ITERS] / (width * lanes * node_count * peers)
-    return ranked, change
+    return pl.pallas_call(
+        functools.partial(end_kernel, width * lanes * node_count * peers),
+        out_shape=(shape((width, node_count), f32), shape((ITERS,), f32)),
+        in_specs=[WHOLE, WHOLE],
+        out_specs=(pl.BlockSpec(memory_space=pltpu.HBM),) * 2,
+        scratch_shapes=[VMEM((ITERS,), f32), pltpu.SemaphoreType.DMA((2,))],
+        compiler_params=LIMIT,
+        name="end",
+    )(theirs, pltpu.with_memory_space_constraint(ranked, VMEM))
 
 
 def solution(mesh):

time: 59.1 us -> 58.4 us (0.988)
    pallas_call x4, Pallas kernels: 7.23 us -> 6.46 us  [shards(): pl.pallas_call(lambda *refs, i=i: step_kernel(i, targets, refs), out_shap...]
    pallas_call x0 -> x1, Pallas kernels: none -> 0.67 us  [shards(): pl.pallas_call(functools.partial(end_kernel, width * lanes * node_count *...]
where the time goes in v4:
time: 58.4 us; the launch traced here: 58.1 us
  blocking collectives  49.2 us (84%)
  Pallas kernels  8.25 us (14%)
  between operations  0.67 us (1%)
    all_to_all x4, blocking collectives, shards(): lax.all_to_all(outgoing.reshape(peers, -1, 1, tile), 'rows', split_axis=0...  37.4 us
    all_to_all x1, blocking collectives, shards(): lax.all_to_all(sums, ('rows', 'feat'), split_axis=0, concat_axis=0, tiled...  11.8 us
    pallas_call x4, Pallas kernels, shards(): pl.pallas_call(lambda *refs, i=i: step_kernel(i, targets, refs), out_shap...  6.46 us

profile of v4, /device:TPU:0, one launch (start us, length us, event | category | flops | bytes accessed | tf_op | source)
XLA Modules:
  0.0 58.1 jit_solution(2037654099709531885)
XLA Ops:
  0.6 0.0 copy-start
  0.6 1.1 %begin.1 = (f32[8,32,128]{2,1,0:T(8,128)S(1)}, f32[200,128]{1,0:T(8,128)S(1)}, s32[128]{0:T(128)S(4)}, s32[8]{0:T(128)S(4)}) custom-call(f32[25,1024]{1,0:T(8,128)} %features_ref.1, s32[128]{0:T(128)} %slot_in_ref.1, s32[8]{0:T(128)} %bitcast.23), custom_call_target="tpu_custom_call" | custom-call | flops 20000000000 | bytes 20000000 | tf_op jit(solution)/shard_map/begin/pallas_call | solution.py:162
  1.8 11.4 %all_to_all.31 = f32[8,25,1,128]{3,2,1,0:T(1,128)S(1)} all-to-all(f32[8,25,1,128]{3,2,1,0:T(1,128)S(1)} %bitcast.20), channel_id=1, replica_groups={{20,24,16,12,28,8,4,0},{21,25,17,13,29,9,5,1},{22,26,18,14,30,10,6,2},{..., dimensions={0} | all-to-all | bytes 204800 | tf_op jit(solution)/shard_map/all_to_all | solution.py:182
  13.2 0.0 copy-done
  13.2 2.4 %step0.1 = (f32[8,32,128]{2,1,0:T(8,128)S(1)}, f32[200,128]{1,0:T(8,128)S(1)}, f32[8,128]{1,0:T(8,128)S(1)}, f32[1,1024]{1,0:T(1,128)S(1)}, bf16[16384,256]{1,0:T(8,128)(2,1)S(1)}) custom-call(f32[8,32,128]{2,1,0:T(8,128)S(1)} %get-tuple-element.19.refs_0_.refs_2_, f32[200,128]{1,0:T(8,128)S(1)} %bitcast.16, ...), custom_call_target="tpu_custom_call" | custom-call | tf_op jit(solution)/shard_map/step0/pallas_call | solution.py:194
  15.6 8.7 %all_to_all.32 = f32[8,25,1,128]{3,2,1,0:T(1,128)S(1)} all-to-all(f32[8,25,1,128]{3,2,1,0:T(1,128)S(1)} %bitcast.17), channel_id=1, replica_groups={{20,24,16,12,28,8,4,0},{21,25,17,13,29,9,5,1},{22,26,18,14,30,10,6,2},{..., dimensions={0} | all-to-all | bytes 204800 | tf_op jit(solution)/shard_map/all_to_all | solution.py:182
  24.2 1.3 %step1.1 = (f32[8,32,128]{2,1,0:T(8,128)S(1)}, f32[200,128]{1,0:T(8,128)S(1)}, f32[8,128]{1,0:T(8,128)S(1)}) custom-call(f32[8,32,128]{2,1,0:T(8,128)S(1)} %get-tuple-element.23.refs_0_, f32[200,128]{1,0:T(8,128)S(1)} %bitcast.14, f32[8,32,128]{2,1,0:T(8,128)S(1)} %get-tuple-element.19.refs_0_.refs_2_, s32[128]{0:T(128)S(4)} %get-tuple-element.21.refs_3_, ...), custom_call_target="tpu_custom_call" | custom-call | tf_op jit(solution)/shard_map/step1/pallas_call | solution.py:194
  25.6 8.7 %all_to_all.33 = f32[8,25,1,128]{3,2,1,0:T(1,128)S(1)} all-to-all(f32[8,25,1,128]{3,2,1,0:T(1,128)S(1)} %bitcast.18), channel_id=1, replica_groups={{20,24,16,12,28,8,4,0},{21,25,17,13,29,9,5,1},{22,26,18,14,30,10,6,2},{..., dimensions={0} | all-to-all | bytes 204800 | tf_op jit(solution)/shard_map/all_to_all | solution.py:182
  34.2 1.3 %step2.1 = (f32[8,32,128]{2,1,0:T(8,128)S(1)}, f32[200,128]{1,0:T(8,128)S(1)}, f32[8,128]{1,0:T(8,128)S(1)}) custom-call(f32[8,32,128]{2,1,0:T(8,128)S(1)} %get-tuple-element.28.refs_0_, f32[200,128]{1,0:T(8,128)S(1)} %bitcast.15, f32[8,32,128]{2,1,0:T(8,128)S(1)} %get-tuple-element.19.refs_0_.refs_2_, s32[128]{0:T(128)S(4)} %get-tuple-element.21.refs_3_, ...), custom_call_target="tpu_custom_call" | custom-call | tf_op jit(solution)/shard_map/step2/pallas_call | solution.py:194
  35.6 8.7 %all_to_all.34 = f32[8,25,1,128]{3,2,1,0:T(1,128)S(1)} all-to-all(f32[8,25,1,128]{3,2,1,0:T(1,128)S(1)} %bitcast.19), channel_id=1, replica_groups={{20,24,16,12,28,8,4,0},{21,25,17,13,29,9,5,1},{22,26,18,14,30,10,6,2},{..., dimensions={0} | all-to-all | bytes 204800 | tf_op jit(solution)/shard_map/all_to_all | solution.py:182
  44.2 1.4 %step3.1 = (f32[25,1024]{1,0:T(8,128)S(1)}, f32[32,128]{1,0:T(8,128)S(1)}) custom-call(f32[8,32,128]{2,1,0:T(8,128)S(1)} %get-tuple-element.31.refs_0_, f32[200,128]{1,0:T(8,128)S(1)} %bitcast.13, f32[8,32,128]{2,1,0:T(8,128)S(1)} %get-tuple-element.19.refs_0_.refs_2_, s32[128]{0:T(128)S(4)} %get-tuple-element.21.refs_3_, s32[8]{0:T(128)S(4)} %get-tuple-element.22.refs_4_, ...), custom_call_target="tpu_custom_call" | custom-call | tf_op jit(solution)/shard_map/step3/pallas_call | solution.py:194
  45.6 11.8 %all_to_all.35 = f32[32,1,128]{2,1,0:T(1,128)S(1)} all-to-all(f32[32,1,128]{2,1,0:T(1,128)S(1)} %bitcast.22), channel_id=1, replica_groups=mesh['rows'=8,'feat'=4] {'rows','feat'}, dimensions={0} | all-to-all | bytes 32768 | tf_op jit(solution)/shard_map/all_to_all | solution.py:210
  57.4 0.7 %end.1 = (f32[25,1024]{1,0:T(8,128)}, f32[4]{0:T(128)}) custom-call(f32[32,128]{1,0:T(8,128)S(1)} %bitcast.21, f32[25,1024]{1,0:T(8,128)S(1)} %get-tuple-element.35.held_ref), custom_call_target="tpu_custom_call" | custom-call | tf_op jit(solution)/shard_map/end/pallas_call | solution.py:211
Async XLA Ops:
  0.6 12.5 %copy-start = (f32[128,128,128]{2,1,0:T(8,128)S(1)}, f32[128,128,128]{2,1,0:T(8,128)}, u32[]{:S(2)}) copy-start(f32[128,128,128]{2,1,0:T(8,128)} %refs_5_.1) | copy-start | bytes 25165828

commit v5 on v4

--- a/solution.py
+++ b/solution.py
@@ -20,7 +20,7 @@
 
 def meeting_order(peers):
     if peers == 8:
-        return [5, 6, 4, 3, 7, 2, 1, 0]
+        return [5, 7, 3, 2, 6, 4, 1, 0]
     middle = peers // 2 + 1
     return sorted(range(peers), key=lambda i: abs(i - middle))
 
@@ -36,16 +36,25 @@
     return high, (v - high.astype(jnp.float32)).astype(jnp.bfloat16)
 
 
-def turn(tiles, by_product):
-    parts = [split(tile) for tile in tiles]
-    if by_product:
-        flat = jnp.concatenate([jnp.concatenate(half, axis=1) for half in zip(*parts)], axis=0)
-        size = flat.shape[1]
-        unit = lax.broadcasted_iota(jnp.int32, (size, size), 0) == lax.broadcasted_iota(jnp.int32, (size, size), 1)
-        unit = unit.astype(jnp.float32).astype(jnp.bfloat16)
-        turned = lax.dot_general(unit, flat, (((1,), (1,)), ((), ())), preferred_element_type=jnp.float32)
-        return turned.astype(jnp.bfloat16)
+def stacked(tiles):
+    return jnp.concatenate([jnp.concatenate(half, axis=1) for half in zip(*(split(tile) for tile in tiles))], axis=0)
+
+
+def turned(tiles):
     return jnp.concatenate([jnp.concatenate(split(tile.T), axis=1) for tile in tiles], axis=0)
+
+
+LATE = (2, 5, 7)
+
+
+def shelves(blocks, per_block):
+    places, filled = {}, {False: 0, True: 0}
+    for b in range(blocks):
+        for t in range(0, per_block, 2):
+            late = t // 2 % 8 in LATE
+            places[b, t] = late, filled[late]
+            filled[late] += min(2, per_block - t)
+    return places, filled[False], filled[True]
 
 
 def begin_kernel(targets, features_ref, slot_in_ref, ids_in_ref, start_ref, outgoing_ref, slot_ref, ids_ref, held_ref, arrived):
@@ -53,9 +62,11 @@
     width = features_ref.shape[0]
     copies = [
         pltpu.make_async_copy(ids_in_ref, ids_ref, arrived.at[0]),
-        pltpu.make_async_copy(features_ref, held_ref, arrived.at[1]),
-        pltpu.make_async_copy(slot_in_ref, slot_ref, arrived.at[2]),
+        pltpu.make_async_copy(slot_in_ref, slot_ref, arrived.at[1]),
     ]
+    for b in range(blocks):
+        r = slice(b * tile, (b + 1) * tile)
+        copies.append(pltpu.make_async_copy(features_ref.at[:, r], held_ref.at[:, r], arrived.at[2 + b]))
     for copy in copies:
         copy.start()
     for copy in copies:
@@ -72,15 +83,18 @@
     refs = list(refs)
     current_ref, received_ref, start_ref, slot_ref, ids_ref = refs[:5]
     views_ref = refs.pop()
-    if first:
-        tiles_ref, next_ref, outgoing_ref, sums_ref, scale_ref, weights_ref = refs[5:]
+    if index == 0:
+        tiles_ref, next_ref, outgoing_ref, sums_ref, scale_ref, early_ref = refs[5:]
+    elif index == 1:
+        scale_ref, early_ref, tiles_ref, past_ref, next_ref, outgoing_ref, sums_ref, late_ref = refs[5:]
     elif last:
-        scale_ref, weights_ref, past_ref, ranked_ref, sums_ref = refs[5:]
+        scale_ref, early_ref, late_ref, past_ref, ranked_ref, sums_ref = refs[5:]
     else:
-        scale_ref, weights_ref, past_ref, next_ref, outgoing_ref, sums_ref = refs[5:]
+        scale_ref, early_ref, late_ref, past_ref, next_ref, outgoing_ref, sums_ref = refs[5:]
     blocks, rows, tile = current_ref.shape
     width = received_ref.shape[0] // len(targets)
-    per_block = weights_ref.shape[0] // (blocks * tile)
+    per_block = slot_ref.shape[0] // blocks
+    places, _, _ = shelves(blocks, per_block)
     for b in range(blocks):
         views_ref[b, 0:rows], views_ref[b, rows:2 * rows] = split(current_ref[b])
     for q, d in enumerate(targets):
@@ -91,16 +105,23 @@
         picked = [views_ref[slot_ref[t]] for t in range(b * per_block, (b + 1) * per_block)]
         lhs = jnp.concatenate(picked, axis=1)
         lhs = jnp.concatenate([lhs, jnp.zeros_like(lhs)], axis=0)
-        if first:
-            s = None
-            for t in range(0, per_block, 2):
-                at = range(b * per_block + t, b * per_block + min(t + 2, per_block))
-                turned = turn([tiles_ref[u] for u in at], by_product=t % 16 == 14)
-                weights_ref[at[0] * tile:(at[-1] + 1) * tile, :] = turned
-                part = jnp.dot(lhs[:, t * tile:(t + 2) * tile], turned, preferred_element_type=jnp.float32)
-                s = part if s is None else s + part
-        else:
-            s = jnp.dot(lhs, weights_ref[b * per_block * tile:(b + 1) * per_block * tile, :], preferred_element_type=jnp.float32)
+        s = None
+        for t in range(0, per_block, 2):
+            n = min(2, per_block - t)
+            late, at = places[b, t]
+            view = lhs[:, t * tile:(t + n) * tile]
+            if late and index == 0:
+                pair = stacked([tiles_ref[b * per_block + t + u] for u in range(n)])
+                part = lax.dot_general(view, pair, (((1,), (1,)), ((), ())), preferred_element_type=jnp.float32)
+            else:
+                shelf_ref = late_ref if late else early_ref
+                if late == (index == 1) and index < 2:
+                    pair = turned([tiles_ref[b * per_block + t + u] for u in range(n)])
+                    shelf_ref[at * tile:(at + n) * tile, :] = pair
+                else:
+                    pair = shelf_ref[at * tile:(at + n) * tile, :]
+                part = jnp.dot(view, pair, preferred_element_type=jnp.float32)
+            s = part if s is None else s + part
         s = s[0:rows] + s[rows:2 * rows]
         s = s[:, 0:tile] + s[:, tile:2 * tile]
         r = slice(b * tile, (b + 1) * tile)
@@ -169,7 +190,7 @@
         ),
         in_specs=[pl.BlockSpec(memory_space=pltpu.HBM)] * 3,
         out_specs=(WHOLE, WHOLE, SCALARS, SCALARS),
-        scratch_shapes=[VMEM(features.shape, f32), pltpu.SemaphoreType.DMA((3,))],
+        scratch_shapes=[VMEM(features.shape, f32), pltpu.SemaphoreType.DMA((2 + blocks,))],
         compiler_params=LIMIT,
         cost_estimate=pl.CostEstimate(flops=20_000_000_000, bytes_accessed=20_000_000, transcendentals=0),
         name="begin",
@@ -177,6 +198,7 @@
 
     current = start
     everyone = peers * lanes
+    _, early_count, late_count = shelves(blocks, tile_count // blocks)
     for i in range(ITERS):
         first, last = i == 0, i == ITERS - 1
         received = lax.all_to_all(
@@ -189,8 +211,10 @@
         else:
             outs = [shape((blocks, rows, tile), f32), shape((halo * width, tile), f32), shape((8, tile), f32)]
         if first:
-            outs += [shape((1, node_count), f32), VMEM((tile_count * tile, 2 * tile), jnp.bfloat16)]
-        kept = (tiles,) if first else (scale, weights, sums)
+            outs += [shape((1, node_count), f32), VMEM((early_count * tile, 2 * tile), jnp.bfloat16)]
+        if i == 1:
+            outs += [VMEM((late_count * tile, 2 * tile), jnp.bfloat16)]
+        kept = (tiles,) if first else (scale, early, tiles, sums) if i == 1 else (scale, early, late, sums)
         got = pl.pallas_call(
             lambda *refs, i=i: step_kernel(i, targets, refs),
             out_shape=tuple(outs),
@@ -201,8 +225,11 @@
             name=f"step{i}",
         )(current, received, start, slot, ids, *kept)
         if first:
-            current, outgoing, sums, scale, weights = got
-            weights = pltpu.with_memory_space_constraint(weights, VMEM)
+            current, outgoing, sums, scale, early = got
+            early = pltpu.with_memory_space_constraint(early, VMEM)
+        elif i == 1:
+            current, outgoing, sums, late = got
+            late = pltpu.with_memory_space_constraint(late, VMEM)
         elif last:
             ranked, sums = got
         else:

time: 58.4 us -> 58.2 us (level)
  no operation moved by 1% of the time
where the time goes in v5:
time: 58.2 us; the launch traced here: 57.9 us
  blocking collectives  49 us (84%)
  Pallas kernels  8.21 us (14%)
  between operations  0.68 us (1%)
    all_to_all x4, blocking collectives, shards(): lax.all_to_all(outgoing.reshape(peers, -1, 1, tile), 'rows', split_axis=0...  37.4 us
    all_to_all x1, blocking collectives, shards(): lax.all_to_all(sums, ('rows', 'feat'), split_axis=0, concat_axis=0, tiled...  11.7 us
    pallas_call x4, Pallas kernels, shards(): pl.pallas_call(lambda *refs, i=i: step_kernel(i, targets, refs), out_shap...  6.45 us

profile of v5, /device:TPU:0, one launch (start us, length us, event | category | flops | bytes accessed | tf_op | source)
XLA Modules:
  0.0 57.9 jit_solution(2612717528261640657)
XLA Ops:
  0.6 0.0 slice-start
  0.6 0.0 slice-start.1
  0.7 1.1 %begin.1 = (f32[8,32,128]{2,1,0:T(8,128)S(1)}, f32[200,128]{1,0:T(8,128)S(1)}, s32[128]{0:T(128)S(4)}, s32[8]{0:T(128)S(4)}) custom-call(f32[25,1024]{1,0:T(8,128)} %features_ref.1, s32[128]{0:T(128)} %slot_in_ref.1, s32[8]{0:T(128)} %bitcast.25), custom_call_target="tpu_custom_call" | custom-call | flops 20000000000 | bytes 20000000 | tf_op jit(solution)/shard_map/begin/pallas_call | solution.py:183
  1.7 11.4 %all_to_all.31 = f32[8,25,1,128]{3,2,1,0:T(1,128)S(1)} all-to-all(f32[8,25,1,128]{3,2,1,0:T(1,128)S(1)} %bitcast.22), channel_id=1, replica_groups={{20,28,12,8,24,16,4,0},{21,29,13,9,25,17,5,1},{22,30,14,10,26,18,6,2},{..., dimensions={0} | all-to-all | bytes 204800 | tf_op jit(solution)/shard_map/all_to_all | solution.py:204
  13.2 0.0 slice-done
  13.2 0.0 slice-done.1
  13.2 2.3 %step0.1 = (f32[8,32,128]{2,1,0:T(8,128)S(1)}, f32[200,128]{1,0:T(8,128)S(1)}, f32[8,128]{1,0:T(8,128)S(1)}, f32[1,1024]{1,0:T(1,128)S(1)}, bf16[10240,256]{1,0:T(8,128)(2,1)S(1)}) custom-call(f32[8,32,128]{2,1,0:T(8,128)S(1)} %get-tuple-element.20.refs_0_.refs_2_, f32[200,128]{1,0:T(8,128)S(1)} %bitcast.18, ...), custom_call_target="tpu_custom_call" | custom-call | tf_op jit(solution)/shard_map/step0/pallas_call | solution.py:218
  15.5 8.7 %all_to_all.32 = f32[8,25,1,128]{3,2,1,0:T(1,128)S(1)} all-to-all(f32[8,25,1,128]{3,2,1,0:T(1,128)S(1)} %bitcast.20), channel_id=1, replica_groups={{20,28,12,8,24,16,4,0},{21,29,13,9,25,17,5,1},{22,30,14,10,26,18,6,2},{..., dimensions={0} | all-to-all | bytes 204800 | tf_op jit(solution)/shard_map/all_to_all | solution.py:204
  24.1 1.4 %step1.1 = (f32[8,32,128]{2,1,0:T(8,128)S(1)}, f32[200,128]{1,0:T(8,128)S(1)}, f32[8,128]{1,0:T(8,128)S(1)}, bf16[6144,256]{1,0:T(8,128)(2,1)S(1)}) custom-call(f32[8,32,128]{2,1,0:T(8,128)S(1)} %get-tuple-element.24.refs_0_, f32[200,128]{1,0:T(8,128)S(1)} %bitcast.17, f32[8,32,128]{2,1,0:T(8,128)S(1)} %get-tuple-element.20.refs_0_.refs_2_, ...), custom_call_target="tpu_custom_call" | custom-call | tf_op jit(solution)/shard_map/step1/pallas_call | solution.py:218
  25.5 8.7 %all_to_all.33 = f32[8,25,1,128]{3,2,1,0:T(1,128)S(1)} all-to-all(f32[8,25,1,128]{3,2,1,0:T(1,128)S(1)} %bitcast.19), channel_id=1, replica_groups={{20,28,12,8,24,16,4,0},{21,29,13,9,25,17,5,1},{22,30,14,10,26,18,6,2},{..., dimensions={0} | all-to-all | bytes 204800 | tf_op jit(solution)/shard_map/all_to_all | solution.py:204
  34.2 1.3 %step2.1 = (f32[8,32,128]{2,1,0:T(8,128)S(1)}, f32[200,128]{1,0:T(8,128)S(1)}, f32[8,128]{1,0:T(8,128)S(1)}) custom-call(f32[8,32,128]{2,1,0:T(8,128)S(1)} %get-tuple-element.29.refs_0_, f32[200,128]{1,0:T(8,128)S(1)} %bitcast.16, f32[8,32,128]{2,1,0:T(8,128)S(1)} %get-tuple-element.20.refs_0_.refs_2_, s32[128]{0:T(128)S(4)} %get-tuple-element.22.refs_3_, ...), custom_call_target="tpu_custom_call" | custom-call | tf_op jit(solution)/shard_map/step2/pallas_call | solution.py:218
  35.5 8.7 %all_to_all.34 = f32[8,25,1,128]{3,2,1,0:T(1,128)S(1)} all-to-all(f32[8,25,1,128]{3,2,1,0:T(1,128)S(1)} %bitcast.21), channel_id=1, replica_groups={{20,28,12,8,24,16,4,0},{21,29,13,9,25,17,5,1},{22,30,14,10,26,18,6,2},{..., dimensions={0} | all-to-all | bytes 204800 | tf_op jit(solution)/shard_map/all_to_all | solution.py:204
  44.2 1.4 %step3.1 = (f32[25,1024]{1,0:T(8,128)S(1)}, f32[32,128]{1,0:T(8,128)S(1)}) custom-call(f32[8,32,128]{2,1,0:T(8,128)S(1)} %get-tuple-element.33.refs_0_, f32[200,128]{1,0:T(8,128)S(1)} %bitcast.15, f32[8,32,128]{2,1,0:T(8,128)S(1)} %get-tuple-element.20.refs_0_.refs_2_, s32[128]{0:T(128)S(4)} %get-tuple-element.22.refs_3_, s32[8]{0:T(128)S(4)} %get-tuple-element.23.refs_4_, ...), custom_call_target="tpu_custom_call" | custom-call | tf_op jit(solution)/shard_map/step3/pallas_call | solution.py:218
  45.6 11.7 %all_to_all.35 = f32[32,1,128]{2,1,0:T(1,128)S(1)} all-to-all(f32[32,1,128]{2,1,0:T(1,128)S(1)} %bitcast.24), channel_id=1, replica_groups=mesh['rows'=8,'feat'=4] {'rows','feat'}, dimensions={0} | all-to-all | bytes 32768 | tf_op jit(solution)/shard_map/all_to_all | solution.py:237
  57.3 0.7 %end.1 = (f32[25,1024]{1,0:T(8,128)}, f32[4]{0:T(128)}) custom-call(f32[32,128]{1,0:T(8,128)S(1)} %bitcast.23, f32[25,1024]{1,0:T(8,128)S(1)} %get-tuple-element.37.held_ref), custom_call_target="tpu_custom_call" | custom-call | tf_op jit(solution)/shard_map/end/pallas_call | solution.py:238
  (1 shorter events, 0.0 us)
Async XLA Ops:
  0.6 12.5 %slice-start = ((s8[8388608]{0:T(1024)(128)(4,1)}), s8[4194304]{0:T(1024)(128)(4,1)S(1)}, s32[]{:S(2)}) async-start(s8[8388608]{0:T(1024)(128)(4,1)} %bitcast.13), calls=%async_computation.5 | async-start | bytes 8388608
  0.6 12.5 %slice-start.1 = ((s8[8388608]{0:T(1024)(128)(4,1)}), s8[4194304]{0:T(1024)(128)(4,1)S(1)}, s32[]{:S(2)}) async-start(s8[8388608]{0:T(1024)(128)(4,1)} %bitcast.13), calls=%async_computation.6 | async-start | bytes 8388608

commit v6 on v5

--- a/solution.py
+++ b/solution.py
@@ -68,7 +68,7 @@
         r = slice(b * tile, (b + 1) * tile)
         copies.append(pltpu.make_async_copy(features_ref.at[:, r], held_ref.at[:, r], arrived.at[2 + b]))
     for copy in copies:
-        copy.start()
+        copy.start(priority=1)
     for copy in copies:
         copy.wait()
     for q, d in enumerate(targets):

time: 58.2 us -> 58.2 us (level)
  no operation moved by 1% of the time
where the time goes in v6:
time: 58.2 us; the launch traced here: 57.9 us
  blocking collectives  49 us (84%)
  Pallas kernels  8.2 us (14%)
  between operations  0.68 us (1%)
    all_to_all x4, blocking collectives, shards(): lax.all_to_all(outgoing.reshape(peers, -1, 1, tile), 'rows', split_axis=0...  37.4 us
    all_to_all x1, blocking collectives, shards(): lax.all_to_all(sums, ('rows', 'feat'), split_axis=0, concat_axis=0, tiled...  11.7 us
    pallas_call x4, Pallas kernels, shards(): pl.pallas_call(lambda *refs, i=i: step_kernel(i, targets, refs), out_shap...  6.45 us

profile of v6, /device:TPU:0, one launch (start us, length us, event | category | flops | bytes accessed | tf_op | source)
XLA Modules:
  0.0 57.9 jit_solution(510137526048495713)
XLA Ops:
  0.6 0.0 slice-start
  0.6 0.0 slice-start.1
  0.7 1.1 %begin.1 = (f32[8,32,128]{2,1,0:T(8,128)S(1)}, f32[200,128]{1,0:T(8,128)S(1)}, s32[128]{0:T(128)S(4)}, s32[8]{0:T(128)S(4)}) custom-call(f32[25,1024]{1,0:T(8,128)} %features_ref.1, s32[128]{0:T(128)} %slot_in_ref.1, s32[8]{0:T(128)} %bitcast.25), custom_call_target="tpu_custom_call" | custom-call | flops 20000000000 | bytes 20000000 | tf_op jit(solution)/shard_map/begin/pallas_call | solution.py:183
  1.7 11.4 %all_to_all.31 = f32[8,25,1,128]{3,2,1,0:T(1,128)S(1)} all-to-all(f32[8,25,1,128]{3,2,1,0:T(1,128)S(1)} %bitcast.22), channel_id=1, replica_groups={{20,28,12,8,24,16,4,0},{21,29,13,9,25,17,5,1},{22,30,14,10,26,18,6,2},{..., dimensions={0} | all-to-all | bytes 204800 | tf_op jit(solution)/shard_map/all_to_all | solution.py:204
  13.2 0.0 slice-done
  13.2 0.0 slice-done.1
  13.2 2.3 %step0.1 = (f32[8,32,128]{2,1,0:T(8,128)S(1)}, f32[200,128]{1,0:T(8,128)S(1)}, f32[8,128]{1,0:T(8,128)S(1)}, f32[1,1024]{1,0:T(1,128)S(1)}, bf16[10240,256]{1,0:T(8,128)(2,1)S(1)}) custom-call(f32[8,32,128]{2,1,0:T(8,128)S(1)} %get-tuple-element.20.refs_0_.refs_2_, f32[200,128]{1,0:T(8,128)S(1)} %bitcast.18, ...), custom_call_target="tpu_custom_call" | custom-call | tf_op jit(solution)/shard_map/step0/pallas_call | solution.py:218
  15.5 8.7 %all_to_all.32 = f32[8,25,1,128]{3,2,1,0:T(1,128)S(1)} all-to-all(f32[8,25,1,128]{3,2,1,0:T(1,128)S(1)} %bitcast.20), channel_id=1, replica_groups={{20,28,12,8,24,16,4,0},{21,29,13,9,25,17,5,1},{22,30,14,10,26,18,6,2},{..., dimensions={0} | all-to-all | bytes 204800 | tf_op jit(solution)/shard_map/all_to_all | solution.py:204
  24.1 1.4 %step1.1 = (f32[8,32,128]{2,1,0:T(8,128)S(1)}, f32[200,128]{1,0:T(8,128)S(1)}, f32[8,128]{1,0:T(8,128)S(1)}, bf16[6144,256]{1,0:T(8,128)(2,1)S(1)}) custom-call(f32[8,32,128]{2,1,0:T(8,128)S(1)} %get-tuple-element.24.refs_0_, f32[200,128]{1,0:T(8,128)S(1)} %bitcast.17, f32[8,32,128]{2,1,0:T(8,128)S(1)} %get-tuple-element.20.refs_0_.refs_2_, ...), custom_call_target="tpu_custom_call" | custom-call | tf_op jit(solution)/shard_map/step1/pallas_call | solution.py:218
  25.5 8.7 %all_to_all.33 = f32[8,25,1,128]{3,2,1,0:T(1,128)S(1)} all-to-all(f32[8,25,1,128]{3,2,1,0:T(1,128)S(1)} %bitcast.19), channel_id=1, replica_groups={{20,28,12,8,24,16,4,0},{21,29,13,9,25,17,5,1},{22,30,14,10,26,18,6,2},{..., dimensions={0} | all-to-all | bytes 204800 | tf_op jit(solution)/shard_map/all_to_all | solution.py:204
  34.2 1.3 %step2.1 = (f32[8,32,128]{2,1,0:T(8,128)S(1)}, f32[200,128]{1,0:T(8,128)S(1)}, f32[8,128]{1,0:T(8,128)S(1)}) custom-call(f32[8,32,128]{2,1,0:T(8,128)S(1)} %get-tuple-element.29.refs_0_, f32[200,128]{1,0:T(8,128)S(1)} %bitcast.16, f32[8,32,128]{2,1,0:T(8,128)S(1)} %get-tuple-element.20.refs_0_.refs_2_, s32[128]{0:T(128)S(4)} %get-tuple-element.22.refs_3_, ...), custom_call_target="tpu_custom_call" | custom-call | tf_op jit(solution)/shard_map/step2/pallas_call | solution.py:218
  35.5 8.7 %all_to_all.34 = f32[8,25,1,128]{3,2,1,0:T(1,128)S(1)} all-to-all(f32[8,25,1,128]{3,2,1,0:T(1,128)S(1)} %bitcast.21), channel_id=1, replica_groups={{20,28,12,8,24,16,4,0},{21,29,13,9,25,17,5,1},{22,30,14,10,26,18,6,2},{..., dimensions={0} | all-to-all | bytes 204800 | tf_op jit(solution)/shard_map/all_to_all | solution.py:204
  44.2 1.4 %step3.1 = (f32[25,1024]{1,0:T(8,128)S(1)}, f32[32,128]{1,0:T(8,128)S(1)}) custom-call(f32[8,32,128]{2,1,0:T(8,128)S(1)} %get-tuple-element.33.refs_0_, f32[200,128]{1,0:T(8,128)S(1)} %bitcast.15, f32[8,32,128]{2,1,0:T(8,128)S(1)} %get-tuple-element.20.refs_0_.refs_2_, s32[128]{0:T(128)S(4)} %get-tuple-element.22.refs_3_, s32[8]{0:T(128)S(4)} %get-tuple-element.23.refs_4_, ...), custom_call_target="tpu_custom_call" | custom-call | tf_op jit(solution)/shard_map/step3/pallas_call | solution.py:218
  45.6 11.7 %all_to_all.35 = f32[32,1,128]{2,1,0:T(1,128)S(1)} all-to-all(f32[32,1,128]{2,1,0:T(1,128)S(1)} %bitcast.24), channel_id=1, replica_groups=mesh['rows'=8,'feat'=4] {'rows','feat'}, dimensions={0} | all-to-all | bytes 32768 | tf_op jit(solution)/shard_map/all_to_all | solution.py:237
  57.3 0.7 %end.1 = (f32[25,1024]{1,0:T(8,128)}, f32[4]{0:T(128)}) custom-call(f32[32,128]{1,0:T(8,128)S(1)} %bitcast.23, f32[25,1024]{1,0:T(8,128)S(1)} %get-tuple-element.37.held_ref), custom_call_target="tpu_custom_call" | custom-call | tf_op jit(solution)/shard_map/end/pallas_call | solution.py:238
  (1 shorter events, 0.0 us)
Async XLA Ops:
  0.6 12.5 %slice-start = ((s8[8388608]{0:T(1024)(128)(4,1)}), s8[4194304]{0:T(1024)(128)(4,1)S(1)}, s32[]{:S(2)}) async-start(s8[8388608]{0:T(1024)(128)(4,1)} %bitcast.13), calls=%async_computation.5 | async-start | bytes 8388608
  0.6 12.5 %slice-start.1 = ((s8[8388608]{0:T(1024)(128)(4,1)}), s8[4194304]{0:T(1024)(128)(4,1)S(1)}, s32[]{:S(2)}) async-start(s8[8388608]{0:T(1024)(128)(4,1)} %bitcast.13), calls=%async_computation.6 | async-start | bytes 8388608

commit v7 on v6

--- a/solution.py
+++ b/solution.py
@@ -69,13 +69,14 @@
         copies.append(pltpu.make_async_copy(features_ref.at[:, r], held_ref.at[:, r], arrived.at[2 + b]))
     for copy in copies:
         copy.start(priority=1)
-    for copy in copies:
+    for copy in copies[:1] + copies[2:]:
         copy.wait()
     for q, d in enumerate(targets):
         at = pl.multiple_of(ids_ref[d] * tile, tile)
         outgoing_ref[q * width:(q + 1) * width, :] = held_ref[:, pl.ds(at, tile)]
     for b in range(blocks):
         start_ref[b] = framed(held_ref[:, b * tile:(b + 1) * tile], rows)
+    copies[1].wait()
 
 
 def step_kernel(index, targets, refs):

time: 58.2 us -> 58.2 us (level)
  no operation moved by 1% of the time
where the time goes in v7:
time: 58.2 us; the launch traced here: 57.9 us
  blocking collectives  49 us (84%)
  Pallas kernels  8.21 us (14%)
  between operations  0.68 us (1%)
    all_to_all x4, blocking collectives, shards(): lax.all_to_all(outgoing.reshape(peers, -1, 1, tile), 'rows', split_axis=0...  37.4 us
    all_to_all x1, blocking collectives, shards(): lax.all_to_all(sums, ('rows', 'feat'), split_axis=0, concat_axis=0, tiled...  11.7 us
    pallas_call x4, Pallas kernels, shards(): pl.pallas_call(lambda *refs, i=i: step_kernel(i, targets, refs), out_shap...  6.45 us

profile of v7, /device:TPU:0, one launch (start us, length us, event | category | flops | bytes accessed | tf_op | source)
XLA Modules:
  0.0 57.9 jit_solution(12409542134458709262)
XLA Ops:
  0.6 0.0 slice-start
  0.6 0.0 slice-start.1
  0.7 1.1 %begin.1 = (f32[8,32,128]{2,1,0:T(8,128)S(1)}, f32[200,128]{1,0:T(8,128)S(1)}, s32[128]{0:T(128)S(4)}, s32[8]{0:T(128)S(4)}) custom-call(f32[25,1024]{1,0:T(8,128)} %features_ref.1, s32[128]{0:T(128)} %slot_in_ref.1, s32[8]{0:T(128)} %bitcast.25), custom_call_target="tpu_custom_call" | custom-call | flops 20000000000 | bytes 20000000 | tf_op jit(solution)/shard_map/begin/pallas_call | solution.py:184
  1.8 11.4 %all_to_all.31 = f32[8,25,1,128]{3,2,1,0:T(1,128)S(1)} all-to-all(f32[8,25,1,128]{3,2,1,0:T(1,128)S(1)} %bitcast.22), channel_id=1, replica_groups={{20,28,12,8,24,16,4,0},{21,29,13,9,25,17,5,1},{22,30,14,10,26,18,6,2},{..., dimensions={0} | all-to-all | bytes 204800 | tf_op jit(solution)/shard_map/all_to_all | solution.py:205
  13.2 0.0 slice-done
  13.2 0.0 slice-done.1
  13.2 2.3 %step0.1 = (f32[8,32,128]{2,1,0:T(8,128)S(1)}, f32[200,128]{1,0:T(8,128)S(1)}, f32[8,128]{1,0:T(8,128)S(1)}, f32[1,1024]{1,0:T(1,128)S(1)}, bf16[10240,256]{1,0:T(8,128)(2,1)S(1)}) custom-call(f32[8,32,128]{2,1,0:T(8,128)S(1)} %get-tuple-element.20.refs_0_.refs_2_, f32[200,128]{1,0:T(8,128)S(1)} %bitcast.18, ...), custom_call_target="tpu_custom_call" | custom-call | tf_op jit(solution)/shard_map/step0/pallas_call | solution.py:219
  15.5 8.7 %all_to_all.32 = f32[8,25,1,128]{3,2,1,0:T(1,128)S(1)} all-to-all(f32[8,25,1,128]{3,2,1,0:T(1,128)S(1)} %bitcast.20), channel_id=1, replica_groups={{20,28,12,8,24,16,4,0},{21,29,13,9,25,17,5,1},{22,30,14,10,26,18,6,2},{..., dimensions={0} | all-to-all | bytes 204800 | tf_op jit(solution)/shard_map/all_to_all | solution.py:205
  24.1 1.4 %step1.1 = (f32[8,32,128]{2,1,0:T(8,128)S(1)}, f32[200,128]{1,0:T(8,128)S(1)}, f32[8,128]{1,0:T(8,128)S(1)}, bf16[6144,256]{1,0:T(8,128)(2,1)S(1)}) custom-call(f32[8,32,128]{2,1,0:T(8,128)S(1)} %get-tuple-element.24.refs_0_, f32[200,128]{1,0:T(8,128)S(1)} %bitcast.17, f32[8,32,128]{2,1,0:T(8,128)S(1)} %get-tuple-element.20.refs_0_.refs_2_, ...), custom_call_target="tpu_custom_call" | custom-call | tf_op jit(solution)/shard_map/step1/pallas_call | solution.py:219
  25.6 8.7 %all_to_all.33 = f32[8,25,1,128]{3,2,1,0:T(1,128)S(1)} all-to-all(f32[8,25,1,128]{3,2,1,0:T(1,128)S(1)} %bitcast.19), channel_id=1, replica_groups={{20,28,12,8,24,16,4,0},{21,29,13,9,25,17,5,1},{22,30,14,10,26,18,6,2},{..., dimensions={0} | all-to-all | bytes 204800 | tf_op jit(solution)/shard_map/all_to_all | solution.py:205
  34.2 1.3 %step2.1 = (f32[8,32,128]{2,1,0:T(8,128)S(1)}, f32[200,128]{1,0:T(8,128)S(1)}, f32[8,128]{1,0:T(8,128)S(1)}) custom-call(f32[8,32,128]{2,1,0:T(8,128)S(1)} %get-tuple-element.29.refs_0_, f32[200,128]{1,0:T(8,128)S(1)} %bitcast.16, f32[8,32,128]{2,1,0:T(8,128)S(1)} %get-tuple-element.20.refs_0_.refs_2_, s32[128]{0:T(128)S(4)} %get-tuple-element.22.refs_3_, ...), custom_call_target="tpu_custom_call" | custom-call | tf_op jit(solution)/shard_map/step2/pallas_call | solution.py:219
  35.5 8.7 %all_to_all.34 = f32[8,25,1,128]{3,2,1,0:T(1,128)S(1)} all-to-all(f32[8,25,1,128]{3,2,1,0:T(1,128)S(1)} %bitcast.21), channel_id=1, replica_groups={{20,28,12,8,24,16,4,0},{21,29,13,9,25,17,5,1},{22,30,14,10,26,18,6,2},{..., dimensions={0} | all-to-all | bytes 204800 | tf_op jit(solution)/shard_map/all_to_all | solution.py:205
  44.2 1.4 %step3.1 = (f32[25,1024]{1,0:T(8,128)S(1)}, f32[32,128]{1,0:T(8,128)S(1)}) custom-call(f32[8,32,128]{2,1,0:T(8,128)S(1)} %get-tuple-element.33.refs_0_, f32[200,128]{1,0:T(8,128)S(1)} %bitcast.15, f32[8,32,128]{2,1,0:T(8,128)S(1)} %get-tuple-element.20.refs_0_.refs_2_, s32[128]{0:T(128)S(4)} %get-tuple-element.22.refs_3_, s32[8]{0:T(128)S(4)} %get-tuple-element.23.refs_4_, ...), custom_call_target="tpu_custom_call" | custom-call | tf_op jit(solution)/shard_map/step3/pallas_call | solution.py:219
  45.6 11.7 %all_to_all.35 = f32[32,1,128]{2,1,0:T(1,128)S(1)} all-to-all(f32[32,1,128]{2,1,0:T(1,128)S(1)} %bitcast.24), channel_id=1, replica_groups=mesh['rows'=8,'feat'=4] {'rows','feat'}, dimensions={0} | all-to-all | bytes 32768 | tf_op jit(solution)/shard_map/all_to_all | solution.py:238
  57.3 0.7 %end.1 = (f32[25,1024]{1,0:T(8,128)}, f32[4]{0:T(128)}) custom-call(f32[32,128]{1,0:T(8,128)S(1)} %bitcast.23, f32[25,1024]{1,0:T(8,128)S(1)} %get-tuple-element.37.held_ref), custom_call_target="tpu_custom_call" | custom-call | tf_op jit(solution)/shard_map/end/pallas_call | solution.py:239
  (1 shorter events, 0.0 us)
Async XLA Ops:
  0.6 12.5 %slice-start = ((s8[8388608]{0:T(1024)(128)(4,1)}), s8[4194304]{0:T(1024)(128)(4,1)S(1)}, s32[]{:S(2)}) async-start(s8[8388608]{0:T(1024)(128)(4,1)} %bitcast.13), calls=%async_computation.5 | async-start | bytes 8388608
  0.6 12.5 %slice-start.1 = ((s8[8388608]{0:T(1024)(128)(4,1)}), s8[4194304]{0:T(1024)(128)(4,1)S(1)}, s32[]{:S(2)}) async-start(s8[8388608]{0:T(1024)(128)(4,1)} %bitcast.13), calls=%async_computation.6 | async-start | bytes 8388608
